TPU v7x, 128 devices: a whole 4x4x4 slice. The times are simulated.
128 devices in a mesh: seq: 32 (over x, z, core), section: 4 (over y).
Axes of the slice: x: 4, y: 4, z: 4, core: 2. Of those that a mesh axis runs over, the one named last changes fastest.
Arguments:
- grad_top: bfloat16 [4, 16384, 2560], P('section', 'seq'), may hold values from -6 to 6
- in_weight: bfloat16 [2560, 2560], P(('seq', 'section')), may hold values from -0.125 to 0.125
- out_weight: bfloat16 [2560, 2560], P(('seq', 'section')), may hold values from -0.125 to 0.125
- gate_branch: bfloat16 [4, 16384, 2560], P('section', 'seq'), may hold values from -6 to 6
- write_vec: bfloat16 [4, 16384, 128], P('section', 'seq'), may hold values from -0.59765625 to 0.59765625
- read_vec: bfloat16 [4, 16384, 128], P('section', 'seq'), may hold values from -6 to 6
- log_decay: float32 [4, 40, 16384], P('section', None, 'seq'), may hold values from -1 to 0
- step_size: float32 [4, 40, 16384], P('section', None, 'seq'), may hold values from 0.005 to 0.05
- skip_gain: float32 [40], replicated, may hold values from 0.5 to 1.5
- visual_pos: int32 [4, 32, 64], P('section', 'seq'), may hold values from 0 to 511, as said below
- visual_count: int32 [4, 32], P('section'), may hold values from 2 to 64, as said below
- visual_owner: int32 [4, 32, 64], P('section'), may hold values from 0 to 31, as said below
- visual_patch: int32 [4, 32, 64], P('section'), may hold values from 0 to 63, as said below
Outputs:
- layer_grads: bfloat16 [4, 16384, 2560], P('section', 'seq')
- patch_grads: bfloat16 [4, 2048, 2560], P('section', 'seq')
Inputs may be any that keep to these rules, and one draw needn't show every extreme that they name: `visual_pos`: the 64 positions of one shard are distinct; only the first visual_count of them hold visual tokens. `visual_count`: in every sequence some shard has all 64 slots live. `visual_owner`: of the slots of one shard at most 2 name one owner; in every sequence one owner is named by 2 live slots of every shard. `visual_patch`: slots of one sequence that name the same owner name distinct patches.
All inputs are finite; a program needn't handle non-finite values.
Results may differ from a plain program's by a relative error of at most 0.014.
Values may be sent and summed in bfloat16 or wider, within the bound.
No kernel may reach another device: no remote copies, remote signals or barrier semaphores. Data moves between devices by JAX's collectives and lax.ppermute only.
A program may use at most 192 MiB of HBM per device.

v0:
```python
import jax
import jax.numpy as jnp
from jax import lax
from jax.sharding import Mesh
from jax.sharding import PartitionSpec as P

GROUP = 256
CAP = 2
SEQ = ("seq_0", "seq_1", "seq_2")
SEQ_SECTION = ("seq_0", "seq_1", "seq_2", "section")


def sent_together(arrays, axis, dim, along):
    ends, at = ([], 0)
    for a in arrays[:-1]:
        at += a.shape[along]
        ends.append(at)
    both = jnp.concatenate(arrays, axis=along)
    return tuple(jnp.split(lax.all_gather(both, axis, axis=dim, tiled=True), ends, axis=along))


def nothing_yet(x, identity):
    return jax.tree.map(
        lambda a, e: jnp.broadcast_to(jnp.asarray(e, a.dtype), a.shape), x, identity
    )


def entering(x, axes, combine, identity):
    before = start = nothing_yet(x, identity)
    subtotal = x
    for axis in reversed(axes):
        length, index = (lax.axis_size(axis), lax.axis_index(axis))
        pieces = jax.tree.map(
            lambda part, kind: lax.all_gather(part.astype(kind), axis),
            subtotal,
            (jnp.bfloat16, jnp.bfloat16),
        )
        inside, subtotal = (start, start)
        for k in reversed(range(length)):
            passed = k > index
            subtotal = combine(
                subtotal, jax.tree.map(lambda part, own: part[k].astype(own.dtype), pieces, x)
            )
            inside = jax.tree.map(lambda new, old: jnp.where(passed, new, old), subtotal, inside)
        before = combine(inside, before)
    return before


def combine_tail(earlier_part, later_part):
    return (
        later_part[0] + earlier_part[0],
        later_part[1] + jnp.exp(later_part[0])[:, None, None] * earlier_part[1],
    )


def body(
    grad_top,
    in_weight,
    out_weight,
    gate_branch,
    write_vec,
    read_vec,
    log_decay,
    step_size,
    skip_gain,
    visual_pos,
    visual_count,
    visual_owner,
    visual_patch,
):
    seq_count = lax.axis_size(SEQ)
    seq_index = lax.axis_index(SEQ)
    grad_rows = grad_top[0]
    tok_rows, model_width = grad_rows.shape
    head_count = log_decay.shape[1]
    inner_width = gate_branch.shape[2]
    head_size = inner_width // head_count
    state_width = write_vec.shape[2]
    slot_count = visual_owner.shape[2]
    w_in_full, w_out_full = sent_together((in_weight, out_weight), SEQ_SECTION, 0, 1)
    out_value = jnp.dot(grad_rows, w_out_full, preferred_element_type=jnp.float32)
    block_len = min(GROUP, tok_rows)
    block_total = tok_rows // block_len
    gated = out_value * jax.nn.silu(gate_branch[0].astype(jnp.float32))
    gated_blocks = gated.reshape(block_total, block_len, head_count, head_size)
    write_blocks = write_vec[0].astype(jnp.float32).reshape(block_total, block_len, state_width)
    read_blocks = read_vec[0].astype(jnp.float32).reshape(block_total, block_len, state_width)
    decay_blocks = log_decay[0].reshape(head_count, block_total, block_len).transpose(1, 0, 2)
    step_blocks = step_size[0].reshape(head_count, block_total, block_len).transpose(1, 0, 2)
    cum_blocks = jnp.cumsum(decay_blocks, axis=2)
    scaled = gated_blocks * jnp.exp(cum_blocks).transpose(0, 2, 1)[:, :, :, None]
    contrib_blocks = jnp.einsum("cshp,csn->chpn", scaled, read_blocks)
    block_decays = cum_blocks[:, :, -1]
    leading = jnp.cumsum(block_decays, axis=0) - block_decays
    device_contrib = jnp.einsum("ch,chpn->hpn", jnp.exp(leading), contrib_blocks)
    device_decay = jnp.sum(block_decays, axis=0)
    identity = (jnp.zeros_like(device_decay), jnp.zeros_like(device_contrib))
    _, inflow = entering((device_decay, device_contrib), SEQ, combine_tail, identity)
    token_locations = jnp.arange(block_len)
    causal = token_locations[None, :] >= token_locations[:, None]

    def block_step(arriving, pieces):
        gated_c, write_c, read_c, cum_c, step_c, contrib_c = pieces
        gram = jnp.dot(write_c, read_c.T)
        log_gap = cum_c[:, None, :] - cum_c[:, :, None]
        mixing = jnp.where(causal[None], jnp.exp(jnp.minimum(log_gap, 0.0)), 0.0) * gram[None]
        within = jnp.einsum("hts,shp->thp", mixing, gated_c)
        tail_decay = jnp.exp(cum_c[:, -1:] - cum_c).T
        from_later = jnp.einsum("hpn,tn->thp", arriving, write_c) * tail_decay[:, :, None]
        inner_c = step_c.T[:, :, None] * (within + from_later) + skip_gain[None, :, None] * gated_c
        leaving = contrib_c + jnp.exp(cum_c[:, -1])[:, None, None] * arriving
        return (leaving, inner_c)

    _, inner_blocks = lax.scan(
        block_step,
        inflow,
        (gated_blocks, write_blocks, read_blocks, cum_blocks, step_blocks, contrib_blocks),
        reverse=True,
    )
    inner_grad = inner_blocks.reshape(tok_rows, inner_width).astype(jnp.bfloat16)
    back = lax.dot_general(
        inner_grad, w_in_full, (((1,), (1,)), ((), ())), preferred_element_type=jnp.float32
    )
    result = (grad_rows.astype(jnp.float32) + back).astype(jnp.bfloat16)
    own_rows = result[visual_pos[0, 0]]
    owner_row = visual_owner[0]
    patch_row = visual_patch[0]
    count_row = visual_count[0]
    slot_ids = jnp.arange(slot_count)
    live_slot = slot_ids[None, :] < count_row[:, None]
    earlier_slot = slot_ids[None, :] < slot_ids[:, None]
    same_owner = (
        (owner_row[:, :, None] == owner_row[:, None, :])
        & live_slot[:, None, :]
        & earlier_slot[None]
    )
    rank_row = jnp.sum(same_owner.astype(jnp.int32), axis=2)
    own_owner = lax.dynamic_index_in_dim(owner_row, seq_index, 0, keepdims=False)
    own_rank = lax.dynamic_index_in_dim(rank_row, seq_index, 0, keepdims=False)
    own_live = lax.dynamic_index_in_dim(live_slot, seq_index, 0, keepdims=False)
    destination = own_owner * CAP + own_rank
    send_columns = jnp.arange(seq_count * CAP)
    send_map = ((send_columns[:, None] == destination[None, :]) & own_live[None, :]).astype(
        jnp.bfloat16
    )
    send_rows = jnp.dot(send_map, own_rows, preferred_element_type=jnp.float32).astype(jnp.bfloat16)
    send_rows = send_rows.reshape(seq_count, CAP, model_width)
    landed = lax.all_to_all(send_rows, SEQ, split_axis=0, concat_axis=0, tiled=True)
    mine_mask = live_slot & (owner_row == seq_index)
    column = jnp.arange(seq_count)[:, None] * CAP + rank_row
    patch_count = seq_count * CAP
    patch_hit = (
        (patch_row.reshape(-1)[:, None] == jnp.arange(patch_count)[None, :])
        & mine_mask.reshape(-1)[:, None]
    ).astype(jnp.bfloat16)
    column_hit = (column.reshape(-1)[:, None] == send_columns[None, :]).astype(jnp.bfloat16)
    select = lax.dot_general(
        patch_hit, column_hit, (((0,), (0,)), ((), ())), preferred_element_type=jnp.float32
    ).astype(jnp.bfloat16)
    patches = jnp.dot(
        select, landed.reshape(seq_count * CAP, model_width), preferred_element_type=jnp.float32
    ).astype(jnp.bfloat16)
    return (result[None], patches[None])


def solution(mesh):
    finer = Mesh(
        mesh.devices.reshape(4, 4, 2, mesh.shape["section"]), ("seq_0", "seq_1", "seq_2", "section")
    )
    return jax.shard_map(
        body,
        mesh=finer,
        in_specs=(
            P("section", SEQ, None),
            P(SEQ_SECTION, None),
            P(SEQ_SECTION, None),
            P("section", SEQ, None),
            P("section", SEQ, None),
            P("section", SEQ, None),
            P("section", None, SEQ),
            P("section", None, SEQ),
            P(),
            P("section", SEQ, None),
            P("section", None),
            P("section", None, None),
            P("section", None, None),
        ),
        out_specs=(P("section", SEQ, None), P("section", SEQ, None)),
        check_vma=False,
    )
```

profile of v0, /device:TPU:1, one launch (start us, length us, event | category | flops | bytes accessed | tf_op | source)
XLA Modules:
  0.0 339.2 jit_solution(17798494890272251375)
XLA Ops:
  7.2 1.7 maximum_bitcast_fusion
  9.0 0.9 reshape_squeeze.6
  9.9 1.2 reduce-window.6
  11.8 3.0 copy.64
  14.9 103.0 %all-gather.16.cloned.1.call-done = bf16[128,20,5120]{2,1,0:T(8,128)(2,1)} async-done(((bf16[1,20,5120]{2,1,0:T(8,128)(2,1)}), bf16[128,20,5120]{2,1,0:T(8,128)(2,1)}) %all-gather.16.cloned.1.call-update) | async-done | bytes 26214416 | tf_op jit(solution)/shard_map/all_gather | solution.py:19
  117.9 32.8 %reshape.400 = bf16[2560,5120]{1,0:T(8,128)(2,1)} reshape(bf16[128,20,5120]{2,1,0:T(8,128)(2,1)} %all-gather.16.cloned.1.call-done) | data formatting | bytes 52428800
  150.7 13.2 %fusion.36 = f32[512,2560]{0,1:T(8,128)} fusion(bf16[2560,5120]{1,0:T(8,128)(2,1)} %reshape.400, bf16[1,512,2560]{1,2,0:T(8,128)(2,1)S(1)} %copy.64, bf16[1,512,2560]{2,1,0:T(8,128)(2,1)} %param.15), kind=kOutput, calls=%fused_computation.48 | convolution fusion | flops 6718750720 | bytes 23592960 | tf_op jit(solution)/shard_map/dot_general | solution.py:81
  163.9 7.4 %reshape.342 = f32[2,256,40,64]{1,0,3,2:T(2,128)} reshape(f32[512,2560]{0,1:T(8,128)} %fusion.36) | data formatting | bytes 10485760 | tf_op jit(solution)/shard_map/reshape | solution.py:85
  171.3 3.3 fusion.37
  174.7 2.1 fusion.46
  176.8 0.9 convert_element_type.267
  179.4 2.5 all-reduce
  181.9 7.6 %all-gather.14.cloned.1.call-done = bf16[80,64,128]{2,1,0:T(8,128)(2,1)} async-done(((bf16[40,64,128]{2,1,0:T(8,128)(2,1)}), bf16[80,64,128]{2,1,0:T(8,128)(2,1)}) %all-gather.14.cloned.1.call-update) | async-done | bytes 1310736 | tf_op jit(solution)/shard_map/all_gather | solution.py:34
  189.4 2.4 fusion.68
  192.0 8.0 %all-gather.3 = bf16[4,1,40]{2,1,0:T(2,128)(2,1)S(1)} all-gather(bf16[1,1,40]{2,1,0:T(2,128)(2,1)S(1)} %get-tuple-element.328), channel_id=1, replica_groups=mesh['seq_0'=4,'seq_1'=4,'seq_2'=2,'section'=4] {'seq_1'}, dimensions={0}, use_global_device_ids=true | all-gather | bytes 400 | tf_op jit(solution)/shard_map/all_gather | solution.py:34
  200.1 28.1 %all-gather.10.cloned.1.call-done = bf16[4,40,64,128]{3,2,1,0:T(8,128)(2,1)} async-done(((bf16[1,40,64,128]{3,2,1,0:T(8,128)(2,1)}), bf16[4,40,64,128]{3,2,1,0:T(8,128)(2,1)}) %all-gather.10.cloned.1.call-update) | async-done | bytes 2621456 | tf_op jit(solution)/shard_map/all_gather | solution.py:34
  228.2 3.3 fusion.56
  231.6 7.6 %all-gather.4 = bf16[4,1,40]{2,1,0:T(2,128)(2,1)S(1)} all-gather(bf16[1,1,40]{2,1,0:T(2,128)(2,1)S(1)} %get-tuple-element.322), channel_id=1, replica_groups=mesh['seq_0'=4,'seq_1'=4,'seq_2'=2,'section'=4] {'seq_0'}, dimensions={0}, use_global_device_ids=true | all-gather | bytes 400 | tf_op jit(solution)/shard_map/all_gather | solution.py:34
  240.4 6.0 %copy.65 = f32[2,256,40,64]{1,3,2,0:T(8,128)} copy(f32[2,256,40,64]{1,0,3,2:T(2,128)} %reshape.342) | data formatting | bytes 10485760 | tf_op jit(solution)/shard_map/reshape | solution.py:85
  246.3 20.3 %all-gather.12.cloned.1.call-done = bf16[4,40,64,128]{3,2,1,0:T(8,128)(2,1)} async-done(((bf16[1,40,64,128]{3,2,1,0:T(8,128)(2,1)}), bf16[4,40,64,128]{3,2,1,0:T(8,128)(2,1)}) %all-gather.12.cloned.1.call-update) | async-done | bytes 2621456 | tf_op jit(solution)/shard_map/all_gather | solution.py:34
  266.7 5.6 %fusion.52 = f32[40,64,128]{2,1,0:T(8,128)S(1)} fusion(bf16[4,40,64,128]{3,2,1,0:T(8,128)(2,1)} %all-gather.12.cloned.1.call-done, f32[40]{0:T(128)S(1)} %get-tuple-element.329, f32[40]{0:T(128)S(1)} %get-tuple-element.327, f32[40]{0:T(128)S(1)} %get-tuple-element.321, f32[40]{0:T(128)S(1)} %get-tuple-element.319, f32[40]{0:T(128)S(1)} %get-tuple-element.320, ...), kind=kLoop, calls=%fused_computation.75 | loop fusion | flops 13434880 | bytes 7866250 | tf_op jit(solution)/shard_map/add | solution.py:52
  272.3 1.8 broadcast_in_dim.46
  274.1 21.6 %while.17 = (s32[]{:T(128)}, f32[40,64,128]{2,1,0:T(8,128)S(1)}, bf16[2,256,40,64]{1,3,2,0:T(8,128)(2,1)}, f32[2,40,64,128]{3,2,1,0:T(8,128)}, f32[2,40,256]{2,1...) while((s32[]{:T(128)}, f32[40,64,128]{2,1,0:T(8,128)S(1)}, ...), condition=%wide.region_5.6_spmd.clone, body=%wide.region_4.5_spmd.clone.sunk | while | flops 534587392 | bytes 29118064 | solution.py:114
  274.3 5.5 %fusion.142 = f32[40,64,256]{2,1,0:T(8,128)} fusion(f32[256,256]{1,0:T(8,128)S(1)} %fusion.140, f32[40,256]{1,0:T(8,128)S(1)} %fusion.141, pred[256,256]{1,0:T(8,128)(4,1)S(1)} %iota_compare_fusion.9, f32[2,256,40,64]{1,3,2,0:T(8,128)} %get-tuple-element.419, s32[]{:T(128)S(6)} %sub.99), kind=kOutput, calls=%fused_computation.2.clone.1 | convolution fusion | flops 346030080 | bytes 4341764 | tf_op jit(solution)/shard_map/while/body/eval_jaxpr/hts,shp->thp/dot_general | solution.py:107
  280.1 4.4 %bitcast_dynamic-update-slice_fusion.2 = bf16[2,256,40,64]{1,3,2,0:T(8,128)(2,1)} fusion(bf16[2,256,40,64]{1,3,2,0:T(8,128)(2,1)} %get-tuple-element.404, s32[]{:T(128)S(6)} %sub.99, f32[40,64,256]{2,1,0:T(8,128)} %fusion.142, f32[2,256,40,64]{1,3,2,0:T(8,128)} %get-tuple-element.419, f32[40,64,128]{2,1,0:T(8,128)S(1)} %get-tuple-element.403, ...), kind=kOutput, calls=%fused_computation.13.clone.1 | convolution fusion | flops 171048960 | bytes 9324032 | tf_op jit(solution)/shard_map/while/body/eval_jaxpr/hpn,tn->thp/dot_general | solution.py:109
  285.1 5.5 %fusion.142 = f32[40,64,256]{2,1,0:T(8,128)} fusion(f32[256,256]{1,0:T(8,128)S(1)} %fusion.140, f32[40,256]{1,0:T(8,128)S(1)} %fusion.141, pred[256,256]{1,0:T(8,128)(4,1)S(1)} %iota_compare_fusion.9, f32[2,256,40,64]{1,3,2,0:T(8,128)} %get-tuple-element.419, s32[]{:T(128)S(6)} %sub.99), kind=kOutput, calls=%fused_computation.2.clone.1 | convolution fusion | flops 346030080 | bytes 4341764 | tf_op jit(solution)/shard_map/while/body/eval_jaxpr/hts,shp->thp/dot_general | solution.py:107
  290.9 4.4 %bitcast_dynamic-update-slice_fusion.2 = bf16[2,256,40,64]{1,3,2,0:T(8,128)(2,1)} fusion(bf16[2,256,40,64]{1,3,2,0:T(8,128)(2,1)} %get-tuple-element.404, s32[]{:T(128)S(6)} %sub.99, f32[40,64,256]{2,1,0:T(8,128)} %fusion.142, f32[2,256,40,64]{1,3,2,0:T(8,128)} %get-tuple-element.419, f32[40,64,128]{2,1,0:T(8,128)S(1)} %get-tuple-element.403, ...), kind=kOutput, calls=%fused_computation.13.clone.1 | convolution fusion | flops 171048960 | bytes 9324032 | tf_op jit(solution)/shard_map/while/body/eval_jaxpr/hpn,tn->thp/dot_general | solution.py:109
  295.6 4.5 %copy.69 = bf16[2,256,40,64]{1,0,3,2:T(2,128)(2,1)S(1)} copy(bf16[2,256,40,64]{1,3,2,0:T(8,128)(2,1)} %get-tuple-element.219) | data formatting | bytes 5242880 | tf_op jit(solution)/shard_map/convert_element_type | solution.py:120
  300.6 10.7 %add_convert_fusion = bf16[512,2560]{1,0:T(8,128)(2,1)S(1)} fusion(bf16[512,2560]{0,1:T(8,128)(2,1)S(1)} %bitcast.279, bf16[2560,5120]{1,0:T(8,128)(2,1)} %reshape.400, bf16[1,512,2560]{2,1,0:T(8,128)(2,1)} %param.15), kind=kOutput, calls=%fused_computation.49 | convolution fusion | flops 6714818560 | bytes 20971520 | tf_op jit(solution)/shard_map/dot_general | solution.py:121
  313.9 6.7 %all-to-all-start = ((bf16[32,2,2560]{2,1,0:T(2,128)(2,1)}), bf16[32,2,2560]{2,1,0:T(2,128)(2,1)S(1)}, u32[]{:S(2)}, u32[]{:S(2)}) async-start(bf16[32,2,2560]{2,1,0:T(2,128)(2,1)} %reshape.344), calls=%async_computation | async-start | bytes 655360 | tf_op jit(solution)/shard_map/all_to_all | solution.py:148
  321.0 9.2 %all-to-all-done = bf16[32,2,2560]{2,1,0:T(2,128)(2,1)S(1)} async-done(((bf16[32,2,2560]{2,1,0:T(2,128)(2,1)}), bf16[32,2,2560]{2,1,0:T(2,128)(2,1)S(1)}, u32[]{:S(2)}, u32[]{:S(2)}) %all-to-all-start) | async-done | bytes 327712 | tf_op jit(solution)/shard_map/all_to_all | solution.py:148
  330.4 2.3 fusion.43
  (100 shorter events, 8.3 us)
Async XLA Ops:
  7.2 110.7 %all-gather.16.cloned.1.call-start = ((), (), s32[]{:S(2)}) async-start(), calls=%async_computation.4 | async-start | bytes 31703040 | tf_op jit(solution)/shard_map/all_gather | solution.py:19
  8.9 180.5 %all-gather.14.cloned.1.call-start = ((), (), s32[]{:S(2)}) async-start(), calls=%async_computation.3 | async-start | bytes 1966080 | tf_op jit(solution)/shard_map/all_gather | solution.py:34
  163.9 7.4 %copy-start.5 = (bf16[1,512,128]{2,1,0:T(8,128)(2,1)S(1)}, bf16[1,512,128]{2,1,0:T(8,128)(2,1)}, u32[]{:S(2)}) copy-start(bf16[1,512,128]{2,1,0:T(8,128)(2,1)} %param.20) | copy-start | bytes 393220
  174.7 2.1 copy-start
  176.8 1.0 copy-start.12
  177.8 50.4 %all-gather.10.cloned.1.call-start = ((), (), s32[]{:S(2)}) async-start(), calls=%async_computation.1 | async-start | bytes 3276800 | tf_op jit(solution)/shard_map/all_gather | solution.py:34
  191.9 74.8 %all-gather.12.cloned.1.call-start = ((), (), s32[]{:S(2)}) async-start(), calls=%async_computation.2 | async-start | bytes 3276800 | tf_op jit(solution)/shard_map/all_gather | solution.py:34
  228.2 3.3 copy-start.7
  228.2 11.1 %copy-start.10 = (s32[1,32]{1,0:T(1,128)S(1)}, s32[1,32]{1,0:T(1,128)}, u32[]{:S(2)}) copy-start(s32[1,32]{1,0:T(1,128)} %param.25) | copy-start | bytes 388
  228.2 11.2 %copy-start.6 = (s32[1,32,64]{2,1,0:T(8,128)S(1)}, s32[1,32,64]{2,1,0:T(8,128)}, u32[]{:S(2)}) copy-start(s32[1,32,64]{2,1,0:T(8,128)} %param.26) | copy-start | bytes 24580
  228.2 12.1 %copy-start.11 = (s32[1,1,64]{2,1,0:T(1,128)S(1)}, s32[1,1,64]{2,1,0:T(1,128)}, u32[]{:S(2)}) copy-start(s32[1,1,64]{2,1,0:T(1,128)} %param.24) | copy-start | bytes 772
  240.3 26.3 %copy-start.2 = (bf16[80,64,128]{2,1,0:T(8,128)(2,1)S(1)}, bf16[80,64,128]{2,1,0:T(8,128)(2,1)}, u32[]{:S(2)}) copy-start(bf16[80,64,128]{2,1,0:T(8,128)(2,1)} %all-gather.14.cloned.1.call-done) | copy-start | bytes 3932164
  272.2 1.8 copy-start.3
  272.2 1.8 copy-start.9
  280.1 4.5 %copy-start.1 = (f32[2,40,64,128]{3,2,1,0:T(8,128)S(1)}, f32[2,40,64,128]{3,2,1,0:T(8,128)}, u32[]{:S(2)}) copy-start(f32[2,40,64,128]{3,2,1,0:T(8,128)} %get-tuple-element.416) | copy-start | bytes 7864324 | tf_op jit(solution)/shard_map/while
  290.9 4.5 %copy-start.1 = (f32[2,40,64,128]{3,2,1,0:T(8,128)S(1)}, f32[2,40,64,128]{3,2,1,0:T(8,128)}, u32[]{:S(2)}) copy-start(f32[2,40,64,128]{3,2,1,0:T(8,128)} %get-tuple-element.416) | copy-start | bytes 7864324 | tf_op jit(solution)/shard_map/while
  311.3 1.5 copy-start.4
  312.8 8.0 %copy-start.8 = (s32[1,32,64]{2,1,0:T(8,128)S(1)}, s32[1,32,64]{2,1,0:T(8,128)}, u32[]{:S(2)}) copy-start(s32[1,32,64]{2,1,0:T(8,128)} %param.27) | copy-start | bytes 24580
  313.9 16.3 %all-to-all-start = ((bf16[32,2,2560]{2,1,0:T(2,128)(2,1)}), bf16[32,2,2560]{2,1,0:T(2,128)(2,1)S(1)}, u32[]{:S(2)}, u32[]{:S(2)}) async-start(bf16[32,2,2560]{2,1,0:T(2,128)(2,1)} %reshape.344), calls=%async_computation | async-start | bytes 655360 | tf_op jit(solution)/shard_map/all_to_all | solution.py:148
Sparse Core Ops, SparseCore 0:
  11.6 106.3 all-gather.15
  177.9 11.4 all-gather.13
  192.0 36.0 all-gather.9
  231.6 35.0 all-gather.11
where the time goes:
time: 341 us; the launch traced here: 339 us
  waiting for transfers between devices  168 us (49%)
  local copies, waits for them, and re-layouts  61.4 us (18%)
  matrix products  52 us (15%)
  blocking collectives  18.1 us (5%)
  other arithmetic  17.6 us (5%)
  between operations  14.8 us (4%)
  starting transfers between devices  6.87 us (2%)
    all_gather x1, waiting for transfers between devices, sent_together(): lax.all_gather(both, axis, axis=dim, tiled=True)  103 us
    all_gather x3, waiting for transfers between devices, entering(): lax.all_gather(part.astype(kind), axis)  55.9 us
    unnamed x30, local copies, waits for them, and re-layouts  37.8 us
    all_gather x2, blocking collectives, entering(): lax.all_gather(part.astype(kind), axis)  15.6 us
    reshape x2, local copies, waits for them, and re-layouts, body(): gated_blocks = gated.reshape(block_total, block_len, head_count, head_size)  13.4 us
    dot_general x1, matrix products, body(): jnp.dot(grad_rows, w_out_full, preferred_element_type=jnp.float32)  13.2 us
    dot_general x2, matrix products, block_step(): within = jnp.einsum('hts,shp->thp', mixing, gated_c)  10.9 us
    dot_general x1, matrix products, body(): lax.dot_general(inner_grad, w_in_full, (((1,), (1,)), ((), ())), preferre...  10.7 us
  transfers between devices with their start and end apart: 5, of which 5 were waited for; matrix products, arithmetic and copies ran while one was open for 4% of the time, Pallas kernels for 0%

commit v1 on v0

v1 whole, which is shorter than its diff:
```python
import functools
import jax
import jax.numpy as jnp
import numpy as np
from jax import lax
from jax.experimental import pallas as pl
from jax.experimental.pallas import tpu as pltpu
from jax.sharding import Mesh
from jax.sharding import PartitionSpec as P

BLK = 256
CAP = 2
X, Z, C, Y = ("seq_0", "seq_1", "seq_2", "section")
SEQ = (X, Z, C)
ALL = (X, Z, C, Y)
SIZES = (4, 4, 2, 4)
HG = 4


def ring_perm(axis, shift):
    at = ALL.index(axis)
    pairs = []
    for i in range(int(np.prod(SIZES))):
        where = list(np.unravel_index(i, SIZES))
        sign = 1 if where[2] == 0 else -1
        where[at] = (where[at] + sign * shift) % SIZES[at]
        pairs.append((i, int(np.ravel_multi_index(where, SIZES))))
    return pairs


def send(a, axis, shift):
    return lax.ppermute(a, ALL, ring_perm(axis, shift))


def swap_cores(a):
    return lax.ppermute(a, C, [(0, 1), (1, 0)])


def chip_rows(own, other, core, axis=0):
    first = core == 0
    return jnp.concatenate([jnp.where(first, own, other), jnp.where(first, other, own)], axis=axis)


def half_of(a, which, axis):
    width = a.shape[axis] // 2
    return lax.dynamic_slice_in_dim(a, which * width, width, axis)


def factors_kernel(write_ref, read_ref, read_t_ref, row_ref, col_ref, step_ref, mix_ref, rt_ref, wt_ref):
    write = write_ref[...]
    read = read_ref[...]
    gram = lax.dot_general(write, read, (((1,), (1,)), ((), ())), preferred_element_type=jnp.float32)
    write_f = write.astype(jnp.float32)
    read_t = read_t_ref[...].astype(jnp.float32)
    t = lax.broadcasted_iota(jnp.int32, gram.shape, 0)
    s = lax.broadcasted_iota(jnp.int32, gram.shape, 1)
    gram = jnp.where(s >= t, gram, 0.0)
    for h in range(HG):
        row = row_ref[0, 0, h : h + 1, :]
        col = col_ref[0, 0, :, h : h + 1]
        step = step_ref[0, 0, :, h : h + 1]
        decay = jnp.exp(jnp.minimum(row - col, 0.0))
        mix_ref[0, h] = (decay * (gram * step)).astype(jnp.bfloat16)
        rt_ref[0, h] = (read_t * jnp.exp(row)).astype(jnp.bfloat16)
        last = row[:, row.shape[1] - 1 :]
        wt_ref[0, h] = (write_f * (jnp.exp(last - col) * step)).astype(jnp.bfloat16)


def factors(write, read, cum, step):
    heads, blocks, _ = cum.shape
    groups = heads // HG
    n = write.shape[1]
    row = cum.reshape(groups, HG, blocks, BLK).transpose(2, 0, 1, 3)
    col = row.transpose(0, 1, 3, 2)
    step_col = step.reshape(groups, HG, blocks, BLK).transpose(2, 0, 3, 1)
    col_spec = pl.BlockSpec((1, 1, BLK, HG), lambda b, g: (b, g, 0, 0))
    return pl.pallas_call(
        factors_kernel,
        grid=(blocks, groups),
        in_specs=[
            pl.BlockSpec((BLK, n), lambda b, g: (b, 0)),
            pl.BlockSpec((BLK, n), lambda b, g: (b, 0)),
            pl.BlockSpec((n, BLK), lambda b, g: (0, b)),
            pl.BlockSpec((1, 1, HG, BLK), lambda b, g: (b, g, 0, 0)),
            col_spec,
            col_spec,
        ],
        out_specs=[
            pl.BlockSpec((1, HG, BLK, BLK), lambda b, g: (b, g, 0, 0)),
            pl.BlockSpec((1, HG, n, BLK), lambda b, g: (b, g, 0, 0)),
            pl.BlockSpec((1, HG, BLK, n), lambda b, g: (b, g, 0, 0)),
        ],
        out_shape=[
            jax.ShapeDtypeStruct((blocks, heads, BLK, BLK), jnp.bfloat16),
            jax.ShapeDtypeStruct((blocks, heads, n, BLK), jnp.bfloat16),
            jax.ShapeDtypeStruct((blocks, heads, BLK, n), jnp.bfloat16),
        ],
        compiler_params=pltpu.CompilerParams(dimension_semantics=("arbitrary", "arbitrary")),
        cost_estimate=pl.CostEstimate(flops=5 * 10**9, bytes_accessed=22 * 10**6, transcendentals=10**7),
        name="factors",
    )(write, read, read.T, row, col, step_col)


def gated_kernel(place_ref, *refs):
    pieces, (x_ref, gate_ref, rt_ref, total_ref, g_ref, local_ref, state_ref, w_ref, sem) = refs[:8], refs[8:]
    step = pl.program_id(0)
    rows, width = pieces[0].shape[1:]
    pairs = state_ref.shape[0]

    def copies():
        for color in range(2):
            for k2 in range(4):
                for k1 in range(4):
                    at = pl.multiple_of(place_ref[color * 16 + k2 * 4 + k1] * rows, 16)
                    yield pltpu.make_async_copy(
                        pieces[color * 4 + k2].at[k1],
                        w_ref.at[pl.ds(at, rows), pl.ds(color * width, width)],
                        sem.at[color * 16 + k2 * 4 + k1],
                    )

    @pl.when(step == 0)
    def _():
        for copy in copies():
            copy.start()
        state_ref[...] = jnp.zeros_like(state_ref)
        for copy in copies():
            copy.wait()

    value = jnp.dot(x_ref[...], w_ref[...], preferred_element_type=jnp.float32)
    gate = gate_ref[...].astype(jnp.float32)
    gated = (value * (gate / (1.0 + jnp.exp(-gate)))).astype(jnp.bfloat16)
    g_ref[...] = gated
    for p in range(pairs):
        cols = slice(p * 128, (p + 1) * 128)
        low = jnp.dot(rt_ref[0, 2 * p], gated[:, cols], preferred_element_type=jnp.float32)
        high = jnp.dot(rt_ref[0, 2 * p + 1], gated[:, cols], preferred_element_type=jnp.float32)
        lane = lax.broadcasted_iota(jnp.int32, low.shape, 1)
        added = jnp.where(lane < 64, low, high)
        later = state_ref[p]
        local_ref[0, p] = later
        state_ref[p] = added + total_ref[0, :, cols] * later


def gated_and_states(place, pieces, x, gate, rt, total):
    tokens, depth = x.shape
    width = gate.shape[1]
    blocks = tokens // BLK
    pairs = width // 128
    n = rt.shape[2]
    back = lambda i: blocks - 1 - i
    return pl.pallas_call(
        gated_kernel,
        grid_spec=pltpu.PrefetchScalarGridSpec(
            num_scalar_prefetch=1,
            grid=(blocks,),
            in_specs=[pl.BlockSpec(memory_space=pl.ANY)] * 8
            + [
                pl.BlockSpec((BLK, depth), lambda i, s: (back(i), 0)),
                pl.BlockSpec((BLK, width), lambda i, s: (back(i), 0)),
                pl.BlockSpec((1, 2 * pairs, n, BLK), lambda i, s: (back(i), 0, 0, 0)),
                pl.BlockSpec((1, 1, width), lambda i, s: (back(i), 0, 0)),
            ],
            out_specs=[
                pl.BlockSpec((BLK, width), lambda i, s: (back(i), 0)),
                pl.BlockSpec((1, pairs, n, 128), lambda i, s: (back(i), 0, 0, 0)),
                pl.BlockSpec((pairs, n, 128), lambda i, s: (0, 0, 0)),
            ],
            scratch_shapes=[pltpu.VMEM((depth, width), jnp.bfloat16), pltpu.SemaphoreType.DMA((32,))],
        ),
        out_shape=[
            jax.ShapeDtypeStruct((tokens, width), jnp.bfloat16),
            jax.ShapeDtypeStruct((blocks, pairs, n, 128), jnp.float32),
            jax.ShapeDtypeStruct((pairs, n, 128), jnp.float32),
        ],
        compiler_params=pltpu.CompilerParams(
            dimension_semantics=("arbitrary",), vmem_limit_bytes=50 * 2**20
        ),
        cost_estimate=pl.CostEstimate(flops=8 * 10**9, bytes_accessed=24 * 10**6, transcendentals=2 * 10**6),
        name="gated",
    )(place, *pieces, x, gate, rt, total)


def inner_kernel(mix_ref, wt_ref, g_ref, local_ref, inflow_ref, coef_ref, skip_ref, out_ref):
    for p in range(HG // 2):
        cols = slice(p * 128, (p + 1) * 128)
        g = g_ref[:, cols]
        arriving = local_ref[0, p] + coef_ref[0, :, cols] * inflow_ref[p].astype(jnp.float32)
        arriving = arriving.astype(jnp.bfloat16)
        halves = []
        for h in (2 * p, 2 * p + 1):
            halves.append(
                jnp.dot(mix_ref[0, h], g, preferred_element_type=jnp.float32)
                + jnp.dot(wt_ref[0, h], arriving, preferred_element_type=jnp.float32)
            )
        lane = lax.broadcasted_iota(jnp.int32, halves[0].shape, 1)
        own = jnp.where(lane < 64, halves[0], halves[1])
        out_ref[:, cols] = (own + skip_ref[:, cols] * g.astype(jnp.float32)).astype(jnp.bfloat16)


def inner_gradient(mix, wt, gated, local, inflow, coef, skip):
    tokens, width = gated.shape
    blocks, heads = mix.shape[:2]
    n = wt.shape[3]
    groups = heads // HG
    return pl.pallas_call(
        inner_kernel,
        grid=(blocks, groups),
        in_specs=[
            pl.BlockSpec((1, HG, BLK, BLK), lambda b, g: (b, g, 0, 0)),
            pl.BlockSpec((1, HG, BLK, n), lambda b, g: (b, g, 0, 0)),
            pl.BlockSpec((BLK, HG * 64), lambda b, g: (b, g)),
            pl.BlockSpec((1, HG // 2, n, 128), lambda b, g: (b, g, 0, 0)),
            pl.BlockSpec((HG // 2, n, 128), lambda b, g: (g, 0, 0)),
            pl.BlockSpec((1, 1, HG * 64), lambda b, g: (b, 0, g)),
            pl.BlockSpec((1, HG * 64), lambda b, g: (0, g)),
        ],
        out_specs=pl.BlockSpec((BLK, HG * 64), lambda b, g: (b, g)),
        out_shape=jax.ShapeDtypeStruct((tokens, width), jnp.bfloat16),
        compiler_params=pltpu.CompilerParams(dimension_semantics=("arbitrary", "arbitrary")),
        cost_estimate=pl.CostEstimate(flops=6 * 10**9, bytes_accessed=25 * 10**6, transcendentals=0),
        name="inner",
    )(mix, wt, gated, local, inflow, coef, skip)


def body(
    grad_top,
    in_weight,
    out_weight,
    gate_branch,
    write_vec,
    read_vec,
    log_decay,
    step_size,
    skip_gain,
    visual_pos,
    visual_count,
    visual_owner,
    visual_patch,
):
    x_at, z_at, core = lax.axis_index(X), lax.axis_index(Z), lax.axis_index(C)
    seq_count = lax.axis_size(SEQ)
    seq_index = lax.axis_index(SEQ)
    chips = lax.axis_size(X) * lax.axis_size(Z)
    chip = x_at * lax.axis_size(Z) + z_at
    sign = 1 - 2 * core
    grad_rows = grad_top[0]
    tok_rows, model_width = grad_rows.shape

    rows_y = lax.all_gather(jnp.concatenate([out_weight, in_weight], axis=1), Y, axis=0, tiled=True)
    w_out_rows, w_in_rows = rows_y[:, : out_weight.shape[1]], rows_y[:, out_weight.shape[1] :]
    w_in_full = lax.all_gather(w_in_rows, SEQ, axis=0, tiled=True)

    w_mine = half_of(w_out_rows, core, 1)
    w_other = swap_cores(half_of(w_out_rows, 1 - core, 1))
    w_chip = chip_rows(w_mine, w_other, core)
    part = w_chip.shape[1] // 2
    pieces = []
    places = []
    for color, (first, second) in enumerate(((X, Z), (Z, X))):
        own = w_chip[:, color * part : (color + 1) * part]
        plane = jnp.stack([own] + [send(own, first, s) for s in (1, 2, 3)])
        for k2 in range(4):
            pieces.append(plane)
            if k2 < 3:
                plane = send(plane, second, 1)
            for k1 in range(4):
                kx, kz = (k1, k2) if color == 0 else (k2, k1)
                places.append(lax.rem(x_at - sign * kx + 4, 4) * 4 + lax.rem(z_at - sign * kz + 4, 4))
    place = jnp.stack(places).astype(jnp.int32)

    x_chip = chip_rows(grad_rows, swap_cores(grad_rows), core)
    gate_chip = chip_rows(
        half_of(gate_branch[0], core, 1), swap_cores(half_of(gate_branch[0], 1 - core, 1)), core
    )
    vectors = jnp.concatenate([write_vec[0], read_vec[0]], axis=1)
    vectors = chip_rows(vectors, swap_cores(vectors), core)
    n = write_vec.shape[2]
    write, read = vectors[:, :n], vectors[:, n:]
    scalars = jnp.stack([log_decay[0], step_size[0]])
    scalars = chip_rows(half_of(scalars, core, 1), swap_cores(half_of(scalars, 1 - core, 1)), core, axis=2)
    heads = scalars.shape[1]
    blocks = scalars.shape[2] // BLK
    decay, step = scalars.reshape(2, heads, blocks, BLK)
    skip = jnp.repeat(half_of(skip_gain, core, 0), 64)[None]

    cum = jnp.cumsum(decay, axis=2)
    tot = jnp.sum(decay, axis=2)
    lanes = lambda a: jnp.repeat(a, 64, axis=0).T[:, None, :]
    after = jnp.cumsum(tot[:, ::-1], axis=1)[:, ::-1] - tot
    chip_tot = jnp.sum(tot, axis=1)
    all_tot = lax.all_gather(chip_tot, (X, Z), axis=0)
    pairs = heads // 2
    chunk = pairs * n // chips
    mine = (chip * chunk + jnp.arange(chunk)) // n
    chunk_decay = jnp.exp(jnp.repeat(all_tot, 64, axis=1)).reshape(chips, pairs, 128)[:, mine]

    mix, rt, wt = factors(write, read, cum, step)
    gated, local, state = gated_and_states(place, pieces, x_chip, gate_chip, rt, jnp.exp(lanes(tot)))

    share = lax.all_to_all(
        state.astype(jnp.bfloat16).reshape(chips, chunk, 128), (X, Z), 0, 0, tiled=True
    ).astype(jnp.float32)
    run = jnp.zeros((chunk, 128), jnp.float32)
    outs = [None] * chips
    for q in reversed(range(chips)):
        outs[q] = run.astype(jnp.bfloat16)
        run = share[q] + chunk_decay[q] * run
    inflow = lax.all_to_all(jnp.stack(outs), (X, Z), 0, 0, tiled=True).reshape(pairs, n, 128)

    inner_chip = inner_gradient(mix, wt, gated, local, inflow, jnp.exp(lanes(after)), skip)
    inner_mine = half_of(inner_chip, core, 0)
    inner_other = swap_cores(half_of(inner_chip, 1 - core, 0))
    inner = chip_rows(inner_mine, inner_other, core, axis=1)

    owner_row = visual_owner[0]
    patch_row = visual_patch[0]
    count_row = visual_count[0]
    slot_count = owner_row.shape[1]
    slot_ids = jnp.arange(slot_count)
    live_slot = slot_ids[None, :] < count_row[:, None]
    earlier_slot = slot_ids[None, :] < slot_ids[:, None]
    same_owner = (
        (owner_row[:, :, None] == owner_row[:, None, :])
        & live_slot[:, None, :]
        & earlier_slot[None]
    )
    rank_row = jnp.sum(same_owner.astype(jnp.int32), axis=2)
    own_owner = lax.dynamic_index_in_dim(owner_row, seq_index, 0, keepdims=False)
    own_rank = lax.dynamic_index_in_dim(rank_row, seq_index, 0, keepdims=False)
    own_live = lax.dynamic_index_in_dim(live_slot, seq_index, 0, keepdims=False)
    destination = own_owner * CAP + own_rank
    send_columns = jnp.arange(seq_count * CAP)
    send_map = ((send_columns[:, None] == destination[None, :]) & own_live[None, :]).astype(jnp.bfloat16)
    pos_map = (visual_pos[0, 0][:, None] == jnp.arange(tok_rows)[None, :]).astype(jnp.bfloat16)
    take = jnp.dot(send_map, pos_map, preferred_element_type=jnp.float32).astype(jnp.bfloat16)

    def exchange(rows):
        sent = jnp.dot(take, rows, preferred_element_type=jnp.float32).astype(jnp.bfloat16)
        sent = sent.reshape(seq_count, CAP, rows.shape[1])
        return lax.all_to_all(sent, SEQ, 0, 0, tiled=True).reshape(seq_count * CAP, rows.shape[1])

    mine_mask = live_slot & (owner_row == seq_index)
    column = jnp.arange(seq_count)[:, None] * CAP + rank_row
    patch_count = seq_count * CAP
    patch_hit = (
        (patch_row.reshape(-1)[:, None] == jnp.arange(patch_count)[None, :])
        & mine_mask.reshape(-1)[:, None]
    ).astype(jnp.bfloat16)
    column_hit = (column.reshape(-1)[:, None] == send_columns[None, :]).astype(jnp.bfloat16)
    select = lax.dot_general(
        patch_hit, column_hit, (((0,), (0,)), ((), ())), preferred_element_type=jnp.float32
    ).astype(jnp.bfloat16)
    placed = lambda rows: jnp.dot(select, rows, preferred_element_type=jnp.float32)

    def project(rows, base):
        back = lax.dot_general(rows, w_in_full, (((1,), (1,)), ((), ())), preferred_element_type=jnp.float32)
        return (base.astype(jnp.float32) + back).astype(jnp.bfloat16)

    grad_patches = placed(exchange(grad_rows))
    inner_patches = placed(exchange(inner)).astype(jnp.bfloat16)
    result = project(inner, grad_rows)
    patches = project(inner_patches, grad_patches)
    return (result[None], patches[None])


def solution(mesh):
    finer = Mesh(mesh.devices.reshape(SIZES), ALL)
    return jax.shard_map(
        body,
        mesh=finer,
        in_specs=(
            P(Y, SEQ, None),
            P(ALL, None),
            P(ALL, None),
            P(Y, SEQ, None),
            P(Y, SEQ, None),
            P(Y, SEQ, None),
            P(Y, None, SEQ),
            P(Y, None, SEQ),
            P(),
            P(Y, SEQ, None),
            P(Y, None),
            P(Y, None, None),
            P(Y, None, None),
        ),
        out_specs=(P(Y, SEQ, None), P(Y, SEQ, None)),
        check_vma=False,
    )
```

time: 341 us -> 294 us (0.86)
  waiting for transfers between devices: 168 us -> 41.9 us
  Pallas kernels: 0 us -> 58.9 us
  starting transfers between devices: 6.87 us -> 50.1 us
  local copies, waits for them, and re-layouts: 61.4 us -> 23.5 us
  blocking collectives: 18.1 us -> 48 us
  matrix products: 52 us -> 24.5 us
  other arithmetic: 17.6 us -> 30.3 us
    all_gather x4 -> x1, waiting for transfers between devices: 159 us -> 0.02 us  [body(): w_in_full = lax.all_gather(w_in_rows, SEQ, axis=0, tiled=True)]
    pallas_call x0 -> x3, Pallas kernels: none -> 58.9 us  [the longest x1 24.3 us: factors(): pl.pallas_call(factors_kernel, grid=(blocks, groups), in_specs=[pl.BlockS...]
    ppermute x0 -> x18, starting transfers between devices: none -> 33.7 us  [the longest x6 18.8 us: swap_cores(): return lax.ppermute(a, C, [(0, 1), (1, 0)])]
    unnamed x30 -> x50, local copies, waits for them, and re-layouts: 37.8 us -> 4.17 us
    unnamed x1, blocking collectives: 2.45 us -> 33.8 us
    dot_general x12 -> x7, matrix products: 52 us -> 24.5 us  [the longest x2 19.8 us: project(): lax.dot_general(rows, w_in_full, (((1,), (1,)), ((), ())), preferred_elem...]
    ppermute x0 -> x18, waiting for transfers between devices: none -> 24.1 us  [the longest x12 24.1 us: send(): return lax.ppermute(a, ALL, ring_perm(axis, shift))]
    reshape x5 -> x6, local copies, waits for them, and re-layouts: 14.4 us -> 2.03 us  [the longest x2 1.69 us: exchange(): sent = sent.reshape(seq_count, CAP, rows.shape[1])]
  transfers between devices with their start and end apart: 5 -> 23, of which waited for: 5 -> 7; matrix products, arithmetic and copies ran while one was open for 4% -> 19% of each run, Pallas kernels for 0% -> 20%
where the time goes in v1:
time: 294 us; the launch traced here: 293 us
  Pallas kernels  58.9 us (20%)
  starting transfers between devices  50.1 us (17%)
  blocking collectives  48 us (16%)
  waiting for transfers between devices  41.9 us (14%)
  other arithmetic  30.3 us (10%)
  matrix products  24.5 us (8%)
  local copies, waits for them, and re-layouts  23.5 us (8%)
  between operations  15.3 us (5%)
    unnamed x1, blocking collectives  33.8 us
    pallas_call x1, Pallas kernels, factors(): pl.pallas_call(factors_kernel, grid=(blocks, groups), in_specs=[pl.BlockS...  24.3 us
    ppermute x12, waiting for transfers between devices, send(): return lax.ppermute(a, ALL, ring_perm(axis, shift))  24.1 us
    dot_general x2, matrix products, project(): lax.dot_general(rows, w_in_full, (((1,), (1,)), ((), ())), preferred_elem...  19.8 us
    ppermute x6, starting transfers between devices, swap_cores(): return lax.ppermute(a, C, [(0, 1), (1, 0)])  18.8 us
    pallas_call x1, Pallas kernels, inner_gradient(): pl.pallas_call(inner_kernel, grid=(blocks, groups), in_specs=[pl.BlockSpe...  18.4 us
    pallas_call x1, Pallas kernels, gated_and_states(): pl.pallas_call(gated_kernel, grid_spec=pltpu.PrefetchScalarGridSpec(num_s...  16.2 us
    ppermute x12, starting transfers between devices, send(): return lax.ppermute(a, ALL, ring_perm(axis, shift))  15 us
  transfers between devices with their start and end apart: 23, of which 7 were waited for; matrix products, arithmetic and copies ran while one was open for 19% of the time, Pallas kernels for 20%

profile of v1, /device:TPU:1, one launch (start us, length us, event | category | flops | bytes accessed | tf_op | source)
XLA Modules:
  0.0 292.5 jit_solution(7138874811559904874)
XLA Ops:
  8.2 14.2 %all-gather.1 = bf16[4,20,5120]{2,1,0:T(8,128)(2,1)S(1)} all-gather(bf16[1,20,5120]{2,1,0:T(8,128)(2,1)S(1)} %maximum_bitcast_fusion), channel_id=1, replica_groups=mesh['seq_0'=4,'seq_1'=4,'seq_2'=2,'section'=4] {'section'}, dimensions={0}, use_global_device_ids=true | all-gather | bytes 1024000 | tf_op jit(solution)/shard_map/all_gather | solution.py:249
  23.5 2.1 collective-permute-start.2
  31.4 2.3 reduce-window.6
  34.0 3.8 %collective-permute-start.9 = (bf16[160,640]{1,0:T(8,128)(2,1)S(1)}, bf16[160,640]{1,0:T(8,128)(2,1)S(1)}, u32[]{:S(2)}, u32[]{:S(2)}) collective-permute-start(bf16[160,640]{1,0:T(8,128)(2,1)S(1)} %get-tuple-element.38), channel_id=1, source_target_pairs={{0,8},{1,9},{2,10},{3,11},{4,28},{5,29},{6,30},{7,31},{8,16},{9,17... | collective-permute-start | bytes 614408 | tf_op jit(solution)/shard_map/ppermute | solution.py:32
  38.6 11.4 %collective-permute-done.9 = bf16[160,640]{1,0:T(8,128)(2,1)S(1)} collective-permute-done((bf16[160,640]{1,0:T(8,128)(2,1)S(1)}, bf16[160,640]{1,0:T(8,128)(2,1)S(1)}, u32[]{:S(2)}, u32[]{:S(2)}) %collective-permute-start.9) | collective-permute-done | bytes 204832 | tf_op jit(solution)/shard_map/ppermute | solution.py:32
  50.0 2.2 collective-permute-start.3
  53.6 2.3 copy.66
  56.6 2.2 copy.67
  59.2 5.0 %collective-permute-start = (bf16[512,256]{0,1:T(8,128)(2,1)}, bf16[512,256]{0,1:T(8,128)(2,1)S(1)}, u32[]{:S(2)}, u32[]{:S(2)}) collective-permute-start(bf16[512,256]{0,1:T(8,128)(2,1)} %pad_maximum_fusion.8), channel_id=1, source_target_pairs={{0,4},{4,0},{1,5},{5,1},{2,6},{6,2},{3,7},{7,3},{8,12},{12,8},{9,1... | collective-permute-start | bytes 786440 | tf_op jit(solution)/shard_map/ppermute | solution.py:36
  64.3 1.9 pad_maximum_fusion.6.refs_4_
  71.8 24.3 %factors.1 = (bf16[4,20,256,256]{3,2,1,0:T(8,128)(2,1)}, bf16[4,20,128,256]{3,2,1,0:T(8,128)(2,1)}, bf16[4,20,256,128]{3,2,1,0:T(8,128)(2,1)}) custom-call(bf16[1024,128]{1,0:T(8,128)(2,1)} %copy.68.write_ref, bf16[1024,128]{1,0:T(8,128)(2,1)} %copy.69.read_ref, bf16[128,1024]{1,0:T(8,128)(2,1)} %bitcast.100, f32[4,5,4,256]{3,2,1,0:T(4,128)} %bitcast.108, ...), custom_call_target="tpu_custom_call" | custom-call | flops 5000000000 | bytes 22000000 | tf_op jit(solution)/shard_map/factors/pallas_call | solution.py:77
  98.9 2.2 bitcast_select_fusion.1
  102.7 8.8 %collective-permute-done.13.refs_6_ = bf16[4,160,640]{2,1,0:T(8,128)(2,1)S(1)} collective-permute-done((bf16[4,160,640]{2,1,0:T(8,128)(2,1)}, bf16[4,160,640]{2,1,0:T(8,128)(2,1)S(1)}, u32[]{:S(2)}, u32[]{:S(2)}) %collective-permute-start.13) | collective-permute-done | bytes 819232 | tf_op jit(solution)/shard_map/ppermute | solution.py:32
  112.8 2.1 collective-permute-start.8
  114.9 2.9 broadcast_select_fusion.1
  117.8 2.6 pad_maximum_fusion.refs_8_
  120.4 2.6 collective-permute-done.14.refs_7_
  124.3 16.2 %gated.1 = (bf16[1024,1280]{1,0:T(8,128)(2,1)}, f32[4,10,128,128]{3,2,1,0:T(8,128)}, f32[10,128,128]{2,1,0:T(8,128)S(1)}) custom-call(s32[32]{0:T(128)S(1)} %stack.138.place_ref, bf16[4,160,640]{2,1,0:T(8,128)(2,1)S(1)} %pad_maximum_fusion.5.refs_0_, bf16[4,160,640]{2,1,0:T(8,128)(2,1)S(1)} %collective-permute-done.6.refs_1_, ...), custom_call_target="tpu_custom_call" | custom-call | flops 8000000000 | bytes 24000000 | tf_op jit(solution)/shard_map/gated/pallas_call | solution.py:151
  141.2 5.0 %all-to-all-start = ((bf16[16,80,128]{2,1,0:T(8,128)(2,1)}), bf16[16,80,128]{2,1,0:T(8,128)(2,1)S(1)}, u32[]{:S(2)}, u32[]{:S(2)}) async-start(bf16[16,80,128]{2,1,0:T(8,128)(2,1)} %bitcast.35), calls=%async_computation | async-start | bytes 655360 | tf_op jit(solution)/shard_map/all_to_all | solution.py:300
  146.6 33.8 %all-reduce = f32[320]{0:T(512)S(1)} all-reduce(f32[320]{0:T(512)S(1)} %dynamic-update-slice), channel_id=2, replica_groups=mesh['seq_0'=4,'seq_1'=4,'seq_2'=2,'section'=4] {'seq_0','seq_1'}, use_global_device_ids=true, to_apply=%add | all-reduce | flops 320 | bytes 2560
  191.6 3.5 %all-to-all-start.1 = ((bf16[16,80,128]{2,1,0:T(8,128)(2,1)}), bf16[16,80,128]{2,1,0:T(8,128)(2,1)S(1)}, u32[]{:S(2)}, u32[]{:S(2)}) async-start(bf16[16,80,128]{2,1,0:T(8,128)(2,1)} %constant_dynamic-update-slice_fusion.2), calls=%async_computation.1 | async-start | bytes 655360 | tf_op jit(solution)/shard_map/all_to_all | solution.py:308
  197.3 5.5 %all-to-all-done.1 = bf16[16,80,128]{2,1,0:T(8,128)(2,1)S(1)} async-done(((bf16[16,80,128]{2,1,0:T(8,128)(2,1)}), bf16[16,80,128]{2,1,0:T(8,128)(2,1)S(1)}, u32[]{:S(2)}, u32[]{:S(2)}) %all-to-all-start.1) | async-done | bytes 327712 | tf_op jit(solution)/shard_map/all_to_all | solution.py:308
  203.5 18.4 %inner.1 = bf16[1024,1280]{1,0:T(8,128)(2,1)} custom-call(bf16[4,20,256,256]{3,2,1,0:T(8,128)(2,1)} %get-tuple-element.8.mix_ref, bf16[4,20,256,128]{3,2,1,0:T(8,128)(2,1)} %get-tuple-element.9.wt_ref, bf16[1024,1280]{1,0:T(8,128)(2,1)} %get-tuple-element.11.g_ref, f32[4,10,128,128]{3,2,1,0:T(8,128)} %get-tuple-element.12.local_ref, ...), custom_call_target="tpu_custom_call" | custom-call | flops 6000000000 | bytes 25000000 | tf_op jit(solution)/shard_map/inner/pallas_call | solution.py:205
  221.9 2.5 constant_dynamic-slice_fusion.3
  224.4 10.9 %collective-permute-start.17 = (bf16[512,1280]{1,0:T(8,128)(2,1)}, bf16[512,1280]{1,0:T(8,128)(2,1)}, u32[]{:S(2)}, u32[]{:S(2)}) collective-permute-start(bf16[512,1280]{1,0:T(8,128)(2,1)} %constant_dynamic-slice_fusion.3), channel_id=1, source_target_pairs={{0,4},{4,0},{1,5},{5,1},{2,6},{6,2},{3,7},{7,3},{8,12},{12,8},{9,1... | collective-permute-start | bytes 3932168 | tf_op jit(solution)/shard_map/ppermute | solution.py:36
  235.6 2.3 convolution_convert_fusion.1
  238.7 3.9 %all-to-all-start.2 = ((bf16[32,2,2560]{2,1,0:T(2,128)(2,1)}), bf16[32,2,2560]{2,1,0:T(2,128)(2,1)S(1)}, u32[]{:S(2)}, u32[]{:S(2)}) async-start(bf16[32,2,2560]{2,1,0:T(2,128)(2,1)} %reshape.206), calls=%async_computation.2 | async-start | bytes 655360 | tf_op jit(solution)/shard_map/all_to_all | solution.py:340
  247.8 4.4 %all-to-all-done.2 = bf16[32,2,2560]{2,1,0:T(2,128)(2,1)S(1)} async-done(((bf16[32,2,2560]{2,1,0:T(2,128)(2,1)}), bf16[32,2,2560]{2,1,0:T(2,128)(2,1)S(1)}, u32[]{:S(2)}, u32[]{:S(2)}) %all-to-all-start.2) | async-done | bytes 327712 | tf_op jit(solution)/shard_map/all_to_all | solution.py:340
  252.3 3.9 %all-to-all-start.3 = ((bf16[32,2,2560]{2,1,0:T(2,128)(2,1)}), bf16[32,2,2560]{2,1,0:T(2,128)(2,1)S(1)}, u32[]{:S(2)}, u32[]{:S(2)}) async-start(bf16[32,2,2560]{2,1,0:T(2,128)(2,1)} %reshape.208), calls=%async_computation.3 | async-start | bytes 655360 | tf_op jit(solution)/shard_map/all_to_all | solution.py:340
  257.9 7.8 %all-to-all-done.3 = bf16[32,2,2560]{2,1,0:T(2,128)(2,1)S(1)} async-done(((bf16[32,2,2560]{2,1,0:T(2,128)(2,1)}), bf16[32,2,2560]{2,1,0:T(2,128)(2,1)S(1)}, u32[]{:S(2)}, u32[]{:S(2)}) %all-to-all-start.3) | async-done | bytes 327712 | tf_op jit(solution)/shard_map/all_to_all | solution.py:340
  265.8 11.8 %fusion = bf16[1,512,2560]{2,1,0:T(8,128)(2,1)} fusion(bf16[2560,2560]{1,0:T(8,128)(2,1)} %all-gather.4.cloned.1.call-done, bf16[512,1280]{1,0:T(8,128)(2,1)} %copy-done.3, bf16[512,1280]{1,0:T(8,128)(2,1)S(1)} %copy-done.2, bf16[1,512,2560]{2,1,0:T(8,128)(2,1)} %param.13), kind=kOutput, calls=%fused_computation.3 | convolution fusion | flops 6720061440 | bytes 20971520 | tf_op jit(solution)/shard_map/dot_general | solution.py:356
  277.6 8.0 %fusion.2 = bf16[1,64,2560]{2,1,0:T(8,128)(2,1)} fusion(f32[64,2560]{1,0:T(8,128)S(1)} %fusion.52, bf16[2560,2560]{1,0:T(8,128)(2,1)} %all-gather.4.cloned.1.call-done, bf16[64,64]{1,0:T(8,128)(2,1)S(1)} %convolution_convert_fusion.4, bf16[64,2560]{1,0:T(8,128)(2,1)S(1)} %reshape.209), kind=kOutput, calls=%fused_computation.9 | convolution fusion | flops 860323840 | bytes 14426112 | tf_op jit(solution)/shard_map/dot_general | solution.py:356
  (175 shorter events, 46.3 us)
Async XLA Ops:
  7.2 258.6 %all-gather.4.cloned.1.call-start = ((), (), s32[]{:S(2)}) async-start(), calls=%async_computation.4 | async-start | bytes 13516800 | tf_op jit(solution)/shard_map/all_gather | solution.py:251
  8.2 17.4 %copy-start.12 = (f32[1,40,512]{2,1,0:T(8,128)S(1)}, f32[1,40,512]{2,1,0:T(8,128)}, u32[]{:S(2)}) copy-start(f32[1,40,512]{2,1,0:T(8,128)} %param.19) | copy-start | bytes 245764
  8.2 17.4 %copy-start.13 = (f32[1,40,512]{2,1,0:T(8,128)S(1)}, f32[1,40,512]{2,1,0:T(8,128)}, u32[]{:S(2)}) copy-start(f32[1,40,512]{2,1,0:T(8,128)} %param.20) | copy-start | bytes 245764
  23.5 10.4 %collective-permute-start.2 = (bf16[80,1280]{1,0:T(8,128)(2,1)S(1)}, bf16[80,1280]{1,0:T(8,128)(2,1)S(1)}, u32[]{:S(2)}, u32[]{:S(2)}) collective-permute-start(bf16[80,1280]{1,0:T(8,128)(2,1)S(1)} %constant_dynamic-slice_fusion.4), channel_id=1, source_target_pairs={{0,4},{4,0},{1,5},{5,1},{2,6},{6,2},{3,7},{7,3},{8,12},{12,8},{9,1... | collective-permute-start | bytes 614408 | tf_op jit(solution)/shard_map/ppermute | solution.py:36
  25.7 5.4 %collective-permute-start.1 = (f32[2,20,512]{2,1,0:T(8,128)S(1)}, f32[2,20,512]{2,1,0:T(8,128)S(1)}, u32[]{:S(2)}, u32[]{:S(2)}) collective-permute-start(f32[2,20,512]{2,1,0:T(8,128)S(1)} %constant_dynamic-slice_fusion.5), channel_id=1, source_target_pairs={{0,4},{4,0},{1,5},{5,1},{2,6},{6,2},{3,7},{7,3},{8,12},{12,8},{9,1... | collective-permute-start | bytes 245768 | tf_op jit(solution)/shard_map/ppermute | solution.py:36
  27.2 71.7 %collective-permute-start.16 = (bf16[512,1280]{1,0:T(8,128)(2,1)S(1)}, bf16[512,1280]{1,0:T(8,128)(2,1)}, u32[]{:S(2)}, u32[]{:S(2)}) collective-permute-start(bf16[512,1280]{1,0:T(8,128)(2,1)S(1)} %dynamic-slice_bitcast_fusion), channel_id=1, source_target_pairs={{0,4},{4,0},{1,5},{5,1},{2,6},{6,2},{3,7},{7,3},{8,12},{12,8},{9,1... | collective-permute-start | bytes 3932168 | tf_op jit(solution)/shard_map/ppermute | solution.py:36
  27.7 87.2 %collective-permute-start.15 = (bf16[512,2560]{1,0:T(8,128)(2,1)}, bf16[512,2560]{1,0:T(8,128)(2,1)}, u32[]{:S(2)}, u32[]{:S(2)}) collective-permute-start(bf16[512,2560]{1,0:T(8,128)(2,1)} %bitcast), channel_id=1, source_target_pairs={{0,4},{4,0},{1,5},{5,1},{2,6},{6,2},{3,7},{7,3},{8,12},{12,8},{9,1... | collective-permute-start | bytes 7864328 | tf_op jit(solution)/shard_map/ppermute | solution.py:36
  28.1 27.8 %copy-start.5 = (bf16[1,512,128]{1,2,0:T(8,128)(2,1)}, bf16[1,512,128]{1,2,0:T(8,128)(2,1)S(1)}, u32[]{:S(2)}) copy-start(bf16[1,512,128]{1,2,0:T(8,128)(2,1)S(1)} %copy.62) | copy-start | bytes 393220
  34.0 16.0 %collective-permute-start.9 = (bf16[160,640]{1,0:T(8,128)(2,1)S(1)}, bf16[160,640]{1,0:T(8,128)(2,1)S(1)}, u32[]{:S(2)}, u32[]{:S(2)}) collective-permute-start(bf16[160,640]{1,0:T(8,128)(2,1)S(1)} %get-tuple-element.38), channel_id=1, source_target_pairs={{0,8},{1,9},{2,10},{3,11},{4,28},{5,29},{6,30},{7,31},{8,16},{9,17... | collective-permute-start | bytes 614408 | tf_op jit(solution)/shard_map/ppermute | solution.py:32
  37.9 14.3 %collective-permute-start.10 = (bf16[160,640]{1,0:T(8,128)(2,1)S(1)}, bf16[160,640]{1,0:T(8,128)(2,1)S(1)}, u32[]{:S(2)}, u32[]{:S(2)}) collective-permute-start(bf16[160,640]{1,0:T(8,128)(2,1)S(1)} %get-tuple-element.38), channel_id=1, source_target_pairs={{0,16},{1,17},{2,18},{3,19},{4,20},{5,21},{6,22},{7,23},{8,24},{9,... | collective-permute-start | bytes 614408 | tf_op jit(solution)/shard_map/ppermute | solution.py:32
  37.9 14.9 %collective-permute-start.11 = (bf16[160,640]{1,0:T(8,128)(2,1)S(1)}, bf16[160,640]{1,0:T(8,128)(2,1)S(1)}, u32[]{:S(2)}, u32[]{:S(2)}) collective-permute-start(bf16[160,640]{1,0:T(8,128)(2,1)S(1)} %get-tuple-element.38), channel_id=1, source_target_pairs={{0,24},{1,25},{2,26},{3,27},{4,12},{5,13},{6,14},{7,15},{8,0},{9,1... | collective-permute-start | bytes 614408 | tf_op jit(solution)/shard_map/ppermute | solution.py:32
  50.0 9.2 %collective-permute-start.3 = (bf16[160,640]{1,0:T(8,128)(2,1)S(1)}, bf16[160,640]{1,0:T(8,128)(2,1)S(1)}, u32[]{:S(2)}, u32[]{:S(2)}) collective-permute-start(bf16[160,640]{1,0:T(8,128)(2,1)S(1)} %get-tuple-element.39), channel_id=1, source_target_pairs={{0,32},{1,33},{2,34},{3,35},{4,100},{5,101},{6,102},{7,103},{8,40}... | collective-permute-start | bytes 614408 | tf_op jit(solution)/shard_map/ppermute | solution.py:32
  52.2 14.0 %collective-permute-start.4 = (bf16[160,640]{1,0:T(8,128)(2,1)S(1)}, bf16[160,640]{1,0:T(8,128)(2,1)}, u32[]{:S(2)}, u32[]{:S(2)}) collective-permute-start(bf16[160,640]{1,0:T(8,128)(2,1)S(1)} %get-tuple-element.39), channel_id=1, source_target_pairs={{0,64},{1,65},{2,66},{3,67},{4,68},{5,69},{6,70},{7,71},{8,72},{9,... | collective-permute-start | bytes 614408 | tf_op jit(solution)/shard_map/ppermute | solution.py:32
  52.7 13.8 %collective-permute-start.5 = (bf16[160,640]{1,0:T(8,128)(2,1)S(1)}, bf16[160,640]{1,0:T(8,128)(2,1)}, u32[]{:S(2)}, u32[]{:S(2)}) collective-permute-start(bf16[160,640]{1,0:T(8,128)(2,1)S(1)} %get-tuple-element.39), channel_id=1, source_target_pairs={{0,96},{1,97},{2,98},{3,99},{4,36},{5,37},{6,38},{7,39},{8,104},{9... | collective-permute-start | bytes 614408 | tf_op jit(solution)/shard_map/ppermute | solution.py:32
  59.2 9.1 %collective-permute-start = (bf16[512,256]{0,1:T(8,128)(2,1)}, bf16[512,256]{0,1:T(8,128)(2,1)S(1)}, u32[]{:S(2)}, u32[]{:S(2)}) collective-permute-start(bf16[512,256]{0,1:T(8,128)(2,1)} %pad_maximum_fusion.8), channel_id=1, source_target_pairs={{0,4},{4,0},{1,5},{5,1},{2,6},{6,2},{3,7},{7,3},{8,12},{12,8},{9,1... | collective-permute-start | bytes 786440 | tf_op jit(solution)/shard_map/ppermute | solution.py:36
  66.2 29.9 %collective-permute-start.12 = (bf16[4,160,640]{2,1,0:T(8,128)(2,1)}, bf16[4,160,640]{2,1,0:T(8,128)(2,1)}, u32[]{:S(2)}, u32[]{:S(2)}) collective-permute-start(bf16[4,160,640]{2,1,0:T(8,128)(2,1)} %pad_maximum_fusion.6.refs_4_), channel_id=1, source_target_pairs={{0,32},{1,33},{2,34},{3,35},{4,100},{5,101},{6,102},{7,103},{8,40}... | collective-permute-start | bytes 2457608 | tf_op jit(solution)/shard_map/ppermute | solution.py:32
  67.7 29.5 %collective-permute-start.6 = (bf16[4,160,640]{2,1,0:T(8,128)(2,1)S(1)}, bf16[4,160,640]{2,1,0:T(8,128)(2,1)S(1)}, u32[]{:S(2)}, u32[]{:S(2)}) collective-permute-start(bf16[4,160,640]{2,1,0:T(8,128)(2,1)S(1)} %pad_maximum_fusion.5.refs_0_), channel_id=1, source_target_pairs={{0,8},{1,9},{2,10},{3,11},{4,28},{5,29},{6,30},{7,31},{8,16},{9,17... | collective-permute-start | bytes 2457608 | tf_op jit(solution)/shard_map/ppermute | solution.py:32
  96.1 15.4 %collective-permute-start.13 = (bf16[4,160,640]{2,1,0:T(8,128)(2,1)}, bf16[4,160,640]{2,1,0:T(8,128)(2,1)S(1)}, u32[]{:S(2)}, u32[]{:S(2)}) collective-permute-start(bf16[4,160,640]{2,1,0:T(8,128)(2,1)} %collective-permute-done.12.refs_5_), channel_id=1, source_target_pairs={{0,32},{1,33},{2,34},{3,35},{4,100},{5,101},{6,102},{7,103},{8,40}... | collective-permute-start | bytes 2457608 | tf_op jit(solution)/shard_map/ppermute | solution.py:32
  97.1 15.7 %collective-permute-start.7 = (bf16[4,160,640]{2,1,0:T(8,128)(2,1)S(1)}, bf16[4,160,640]{2,1,0:T(8,128)(2,1)S(1)}, u32[]{:S(2)}, u32[]{:S(2)}) collective-permute-start(bf16[4,160,640]{2,1,0:T(8,128)(2,1)S(1)} %collective-permute-done.6.refs_1_), channel_id=1, source_target_pairs={{0,8},{1,9},{2,10},{3,11},{4,28},{5,29},{6,30},{7,31},{8,16},{9,17... | collective-permute-start | bytes 2457608 | tf_op jit(solution)/shard_map/ppermute | solution.py:32
  111.5 11.5 %collective-permute-start.14 = (bf16[4,160,640]{2,1,0:T(8,128)(2,1)S(1)}, bf16[4,160,640]{2,1,0:T(8,128)(2,1)S(1)}, u32[]{:S(2)}, u32[]{:S(2)}) collective-permute-start(bf16[4,160,640]{2,1,0:T(8,128)(2,1)S(1)} %collective-permute-done.13.refs_6_), channel_id=1, source_target_pairs={{0,32},{1,33},{2,34},{3,35},{4,100},{5,101},{6,102},{7,103},{8,40}... | collective-permute-start | bytes 2457608 | tf_op jit(solution)/shard_map/ppermute | solution.py:32
  112.8 11.5 %collective-permute-start.8 = (bf16[4,160,640]{2,1,0:T(8,128)(2,1)S(1)}, bf16[4,160,640]{2,1,0:T(8,128)(2,1)S(1)}, u32[]{:S(2)}, u32[]{:S(2)}) collective-permute-start(bf16[4,160,640]{2,1,0:T(8,128)(2,1)S(1)} %collective-permute-done.7.refs_2_), channel_id=1, source_target_pairs={{0,8},{1,9},{2,10},{3,11},{4,28},{5,29},{6,30},{7,31},{8,16},{9,17... | collective-permute-start | bytes 2457608 | tf_op jit(solution)/shard_map/ppermute | solution.py:32
  124.3 22.0 %copy-start.15 = (s32[1,32]{1,0:T(1,128)S(1)}, s32[1,32]{1,0:T(1,128)}, u32[]{:S(2)}) copy-start(s32[1,32]{1,0:T(1,128)} %param.23) | copy-start | bytes 388
  141.2 40.4 %all-to-all-start = ((bf16[16,80,128]{2,1,0:T(8,128)(2,1)}), bf16[16,80,128]{2,1,0:T(8,128)(2,1)S(1)}, u32[]{:S(2)}, u32[]{:S(2)}) async-start(bf16[16,80,128]{2,1,0:T(8,128)(2,1)} %bitcast.35), calls=%async_computation | async-start | bytes 655360 | tf_op jit(solution)/shard_map/all_to_all | solution.py:300
  181.4 13.8 %copy-start.9 = (s32[1,32,64]{2,1,0:T(8,128)S(1)}, s32[1,32,64]{2,1,0:T(8,128)}, u32[]{:S(2)}) copy-start(s32[1,32,64]{2,1,0:T(8,128)} %param.24) | copy-start | bytes 24580
  191.6 11.2 %all-to-all-start.1 = ((bf16[16,80,128]{2,1,0:T(8,128)(2,1)}), bf16[16,80,128]{2,1,0:T(8,128)(2,1)S(1)}, u32[]{:S(2)}, u32[]{:S(2)}) async-start(bf16[16,80,128]{2,1,0:T(8,128)(2,1)} %constant_dynamic-update-slice_fusion.2), calls=%async_computation.1 | async-start | bytes 655360 | tf_op jit(solution)/shard_map/all_to_all | solution.py:308
  221.9 13.4 %copy-start.19 = (s32[1,1,64]{2,1,0:T(1,128)S(1)}, s32[1,1,64]{2,1,0:T(1,128)}, u32[]{:S(2)}) copy-start(s32[1,1,64]{2,1,0:T(1,128)} %param.22) | copy-start | bytes 772
  224.4 18.6 %copy-start.14 = (s32[1,32,64]{2,1,0:T(8,128)S(1)}, s32[1,32,64]{2,1,0:T(8,128)}, u32[]{:S(2)}) copy-start(s32[1,32,64]{2,1,0:T(8,128)} %param.25) | copy-start | bytes 24580
  224.4 18.7 %copy-start = (bf16[1024,1280]{1,0:T(8,128)(2,1)S(1)}, bf16[1024,1280]{1,0:T(8,128)(2,1)}, u32[]{:S(2)}) copy-start(bf16[1024,1280]{1,0:T(8,128)(2,1)} %inner.1) | copy-start | bytes 7864324
  224.4 18.7 %collective-permute-start.17 = (bf16[512,1280]{1,0:T(8,128)(2,1)}, bf16[512,1280]{1,0:T(8,128)(2,1)}, u32[]{:S(2)}, u32[]{:S(2)}) collective-permute-start(bf16[512,1280]{1,0:T(8,128)(2,1)} %constant_dynamic-slice_fusion.3), channel_id=1, source_target_pairs={{0,4},{4,0},{1,5},{5,1},{2,6},{6,2},{3,7},{7,3},{8,12},{12,8},{9,1... | collective-permute-start | bytes 3932168 | tf_op jit(solution)/shard_map/ppermute | solution.py:36
  238.7 13.5 %all-to-all-start.2 = ((bf16[32,2,2560]{2,1,0:T(2,128)(2,1)}), bf16[32,2,2560]{2,1,0:T(2,128)(2,1)S(1)}, u32[]{:S(2)}, u32[]{:S(2)}) async-start(bf16[32,2,2560]{2,1,0:T(2,128)(2,1)} %reshape.206), calls=%async_computation.2 | async-start | bytes 655360 | tf_op jit(solution)/shard_map/all_to_all | solution.py:340
  247.0 18.8 %copy-start.2 = (bf16[512,1280]{1,0:T(8,128)(2,1)S(1)}, bf16[512,1280]{1,0:T(8,128)(2,1)}, u32[]{:S(2)}) copy-start(bf16[512,1280]{1,0:T(8,128)(2,1)} %copy-done.1) | copy-start | bytes 3932164
  252.3 13.4 %all-to-all-start.3 = ((bf16[32,2,2560]{2,1,0:T(2,128)(2,1)}), bf16[32,2,2560]{2,1,0:T(2,128)(2,1)S(1)}, u32[]{:S(2)}, u32[]{:S(2)}) async-start(bf16[32,2,2560]{2,1,0:T(2,128)(2,1)} %reshape.208), calls=%async_computation.3 | async-start | bytes 655360 | tf_op jit(solution)/shard_map/all_to_all | solution.py:340
  (12 other events, 45.7 us)
Sparse Core Ops, SparseCore 0:
  23.6 83.0 all-gather.3

commit v2 on v1

v2 whole, which is shorter than its diff:
```python
import functools
import jax
import jax.numpy as jnp
import numpy as np
from jax import lax
from jax.experimental import pallas as pl
from jax.experimental.pallas import tpu as pltpu
from jax.sharding import Mesh
from jax.sharding import PartitionSpec as P

BLK = 128
MID = 63
STEP = 256
CAP = 2
X, Z, C, Y = ("seq_0", "seq_1", "seq_2", "section")
SEQ = (X, Z, C)
ALL = (X, Z, C, Y)
SIZES = (4, 4, 2, 4)


def ring_perm(axis, shift):
    at = ALL.index(axis)
    pairs = []
    for i in range(int(np.prod(SIZES))):
        where = list(np.unravel_index(i, SIZES))
        sign = 1 if where[2] == 0 else -1
        where[at] = (where[at] + sign * shift) % SIZES[at]
        pairs.append((i, int(np.ravel_multi_index(where, SIZES))))
    return pairs


def send(a, axis, shift):
    return lax.ppermute(a, ALL, ring_perm(axis, shift))


def swap_cores(a):
    return lax.ppermute(a, C, [(0, 1), (1, 0)])


def chip_rows(own, other, core, axis=0):
    first = core == 0
    return jnp.concatenate([jnp.where(first, own, other), jnp.where(first, other, own)], axis=axis)


def half_of(a, which, axis):
    width = a.shape[axis] // 2
    return lax.dynamic_slice_in_dim(a, which * width, width, axis)


def split(a):
    high = a.astype(jnp.bfloat16).astype(jnp.float32)
    return jnp.concatenate([high, a - high], axis=0).astype(jnp.bfloat16)


def spread(parts, heads_ref):
    return lax.dot_general(
        parts, heads_ref[...], (((0,), (0,)), ((), ())), preferred_element_type=jnp.float32
    )


def decays_kernel(info_ref, decay_ref, step_ref, other_ref, heads_ref, u_ref, v_ref, row_ref, extra_ref):
    heads = decay_ref.shape[0] // 2
    core = info_ref[0]
    first = core == 0
    own_decay = jnp.where(first, decay_ref[:heads], decay_ref[heads:])
    own_step = jnp.where(first, step_ref[:heads], step_ref[heads:])
    blocks = v_ref.shape[0]
    per = blocks // 2
    r = lax.broadcasted_iota(jnp.int32, (BLK, BLK), 0)
    c = lax.broadcasted_iota(jnp.int32, (BLK, BLK), 1)
    tri = (r <= c).astype(jnp.float32)
    lane = lax.broadcasted_iota(jnp.int32, (heads, BLK), 1)
    after = jnp.zeros((heads, 1), jnp.float32)
    for b in reversed(range(blocks)):
        cols = slice((b % per) * BLK, (b % per + 1) * BLK)
        own = core == b // per
        decay = jnp.where(own, own_decay[:, cols], other_ref[:heads, cols])
        step = jnp.where(own, own_step[:, cols], other_ref[heads:, cols])
        cum = jnp.dot(decay, tri, precision=lax.Precision.HIGHEST, preferred_element_type=jnp.float32)
        mid = cum[:, MID : MID + 1]
        tot = cum[:, BLK - 1 :]
        v_ref[b] = split(jnp.exp(cum - mid))
        u_ref[b] = split(jnp.exp(mid - cum) * step)
        rows = jnp.where(
            lane == 0,
            jnp.exp(mid),
            jnp.where(
                lane == 1,
                jnp.exp(tot),
                jnp.where(lane == 2, jnp.exp(tot - mid), jnp.exp(tot - mid) * jnp.exp(after)),
            ),
        )
        row_ref[b] = spread(split(rows), heads_ref)[:8]
        after = after + tot
    eye = lax.broadcasted_iota(jnp.int32, (heads, BLK), 0) == lane
    whole = jnp.sum(jnp.where(eye, jnp.exp(after), 0.0), axis=0, keepdims=True)
    high = whole.astype(jnp.bfloat16).astype(jnp.float32)
    row = lax.broadcasted_iota(jnp.int32, (8, BLK), 0)
    extra_ref[...] = jnp.where(row == 0, high, jnp.where(row == 1, whole - high, 0.0)).astype(jnp.bfloat16)


def decays(info, decay, step, other, heads_map):
    heads = decay.shape[0] // 2
    blocks = 2 * decay.shape[1] // BLK
    vmem = pl.BlockSpec(memory_space=pltpu.VMEM)
    return pl.pallas_call(
        decays_kernel,
        in_specs=[pl.BlockSpec(memory_space=pltpu.SMEM)] + [vmem] * 4,
        out_specs=[vmem] * 4,
        out_shape=[
            jax.ShapeDtypeStruct((blocks, 2 * heads, BLK), jnp.bfloat16),
            jax.ShapeDtypeStruct((blocks, 2 * heads, BLK), jnp.bfloat16),
            jax.ShapeDtypeStruct((blocks, 8, heads_map.shape[1]), jnp.float32),
            jax.ShapeDtypeStruct((8, BLK), jnp.bfloat16),
        ],
        cost_estimate=pl.CostEstimate(flops=10**9, bytes_accessed=10**6, transcendentals=10**5),
        name="decays",
    )(info, decay, step, other, heads_map)


def gated_kernel(info_ref, place_ref, *refs):
    pieces = refs[:8]
    (x_own_ref, x_other_ref, gate_own_ref, gate_other_ref, read_ref, v_ref, row_ref, extra_ref, heads_ref,
     g_ref, gv_ref, local_ref, share_ref, state_ref, w_ref, sem) = refs[8:]
    step = pl.program_id(0)
    core = info_ref[0]
    rows, part = pieces[0].shape[1:]

    def copies():
        for color in range(2):
            for k2 in range(4):
                for k1 in range(4):
                    at = pl.multiple_of(place_ref[color * 16 + k2 * 4 + k1] * rows, 16)
                    yield pltpu.make_async_copy(
                        pieces[color * 4 + k2].at[k1],
                        w_ref.at[pl.ds(at, rows), pl.ds(color * part, part)],
                        sem.at[color * 16 + k2 * 4 + k1],
                    )

    @pl.when(step == 0)
    def _():
        for copy in copies():
            copy.start()
        state_ref[...] = jnp.zeros_like(state_ref)
        for copy in copies():
            copy.wait()

    block = pl.num_programs(0) - 1 - step
    own = (block // 2) == core
    x = jnp.where(own, x_own_ref[...], x_other_ref[...])
    value = jnp.dot(x, w_ref[...], preferred_element_type=jnp.float32)
    gate = jnp.where(own, gate_own_ref[...], gate_other_ref[...]).astype(jnp.float32)
    gated = value * (gate / (1.0 + jnp.exp(-gate)))
    g_ref[...] = gated.astype(jnp.bfloat16)
    for b in reversed(range(STEP // BLK)):
        at = slice(b * BLK, (b + 1) * BLK)
        gv = (gated[at] * spread(v_ref[b], heads_ref)).astype(jnp.bfloat16)
        gv_ref[at] = gv
        added = lax.dot_general(
            read_ref[at], gv, (((0,), (0,)), ((), ())), preferred_element_type=jnp.float32
        )
        later = state_ref[...]
        local_ref[b] = (later * row_ref[b, 2:3]).astype(jnp.bfloat16)
        state_ref[...] = added * row_ref[b, 0:1] + row_ref[b, 1:2] * later

    @pl.when(step == pl.num_programs(0) - 1)
    def _():
        width = state_ref.shape[1]
        for j in range(share_ref.shape[0]):
            share_ref[j, :, :width] = state_ref[j * 8 : (j + 1) * 8].astype(jnp.bfloat16)
            share_ref[j, :, width:] = extra_ref[...]


def gated_and_states(info, place, pieces, x_own, x_other, gate_own, gate_other, read, v, row, extra, heads_map):
    depth = x_own.shape[1]
    width = gate_other.shape[1]
    blocks = v.shape[0]
    n = read.shape[1]
    steps = blocks * BLK // STEP
    per = STEP // BLK
    tokens = blocks * BLK
    chips = n // 8
    back = lambda i: steps - 1 - i

    def own_at(i, s):
        return jnp.where(s[0] == 1, jnp.maximum(1 - i, 0), jnp.minimum(1, steps - 1 - i))

    def other_at(i, s):
        return jnp.where(s[0] == 0, jnp.maximum(1 - i, 0), jnp.minimum(1, steps - 1 - i))

    return pl.pallas_call(
        gated_kernel,
        grid_spec=pltpu.PrefetchScalarGridSpec(
            num_scalar_prefetch=2,
            grid=(steps,),
            in_specs=[pl.BlockSpec(memory_space=pl.ANY)] * 8
            + [
                pl.BlockSpec((STEP, depth), lambda i, s, t: (own_at(i, s), 0)),
                pl.BlockSpec((STEP, depth), lambda i, s, t: (other_at(i, s), 0)),
                pl.BlockSpec((STEP, width), lambda i, s, t: (own_at(i, s), s[0])),
                pl.BlockSpec((STEP, width), lambda i, s, t: (other_at(i, s), 0)),
                pl.BlockSpec((STEP, n), lambda i, s, t: (back(i), 0)),
                pl.BlockSpec((per, *v.shape[1:]), lambda i, s, t: (back(i), 0, 0)),
                pl.BlockSpec((per, 8, width), lambda i, s, t: (back(i), 0, 0)),
                pl.BlockSpec(extra.shape, lambda i, s, t: (0, 0)),
                pl.BlockSpec(heads_map.shape, lambda i, s, t: (0, 0)),
            ],
            out_specs=[
                pl.BlockSpec((STEP, width), lambda i, s, t: (back(i), 0)),
                pl.BlockSpec((STEP, width), lambda i, s, t: (back(i), 0)),
                pl.BlockSpec((per, n, width), lambda i, s, t: (back(i), 0, 0)),
                pl.BlockSpec((chips, 8, width + BLK), lambda i, s, t: (0, 0, 0)),
            ],
            scratch_shapes=[
                pltpu.VMEM((n, width), jnp.float32),
                pltpu.VMEM((depth, width), jnp.bfloat16),
                pltpu.SemaphoreType.DMA((32,)),
            ],
        ),
        out_shape=[
            jax.ShapeDtypeStruct((tokens, width), jnp.bfloat16),
            jax.ShapeDtypeStruct((tokens, width), jnp.bfloat16),
            jax.ShapeDtypeStruct((blocks, n, width), jnp.bfloat16),
            jax.ShapeDtypeStruct((chips, 8, width + BLK), jnp.bfloat16),
        ],
        compiler_params=pltpu.CompilerParams(
            dimension_semantics=("arbitrary",), vmem_limit_bytes=50 * 2**20
        ),
        cost_estimate=pl.CostEstimate(flops=8 * 10**9, bytes_accessed=24 * 10**6, transcendentals=2 * 10**6),
        name="gated",
    )(info, place, *pieces, x_own, x_other, gate_own, gate_other, read, v, row, extra, heads_map)


def suffix_kernel(share_ref, heads_ref, out_ref):
    chips, _, width = out_ref.shape
    heads = heads_ref.shape[0] // 2
    parts = share_ref[:, 0:1, width:].reshape(chips, BLK), share_ref[:, 1:2, width:].reshape(chips, BLK)
    spread_of = lambda a: jnp.dot(a[:, :heads], heads_ref[:heads], preferred_element_type=jnp.float32)
    decay = spread_of(parts[0]) + spread_of(parts[1])
    run = jnp.zeros(out_ref.shape[1:], jnp.float32)
    for q in reversed(range(chips)):
        out_ref[q] = run.astype(jnp.bfloat16)
        run = share_ref[q, :, :width].astype(jnp.float32) + decay[q : q + 1] * run


def suffix(share, heads_map):
    chips, rows, _ = share.shape
    vmem = pl.BlockSpec(memory_space=pltpu.VMEM)
    return pl.pallas_call(
        suffix_kernel,
        in_specs=[vmem, vmem],
        out_specs=vmem,
        out_shape=jax.ShapeDtypeStruct((chips, rows, heads_map.shape[1]), jnp.bfloat16),
        cost_estimate=pl.CostEstimate(flops=10**8, bytes_accessed=10**6, transcendentals=0),
        name="suffix",
    )(share, heads_map)


def inner_kernel(
    info_ref, write_ref, read_ref, u_ref, g_ref, gv_ref, local_ref, inflow_ref, row_ref, skip_ref, heads_ref, out_ref
):
    r = lax.broadcasted_iota(jnp.int32, (BLK, BLK), 0)
    c = lax.broadcasted_iota(jnp.int32, (BLK, BLK), 1)
    for b in range(STEP // BLK):
        at = slice(b * BLK, (b + 1) * BLK)
        write = write_ref[at]
        gram = lax.dot_general(
            write, read_ref[at], (((1,), (1,)), ((), ())), preferred_element_type=jnp.float32
        )
        left = jnp.concatenate([jnp.where(c >= r, gram, 0.0).astype(jnp.bfloat16), write], axis=1)
        arriving = local_ref[b].astype(jnp.float32) + row_ref[b, 3:4] * inflow_ref[...].astype(jnp.float32)
        right = jnp.concatenate([gv_ref[at], arriving.astype(jnp.bfloat16)], axis=0)
        value = jnp.dot(left, right, preferred_element_type=jnp.float32) * spread(u_ref[b], heads_ref)
        out_ref[at] = (value + skip_ref[...] * g_ref[at].astype(jnp.float32)).astype(jnp.bfloat16)


def inner_gradient(info, write, read, u, gated, gated_v, local, inflow, row, skip, heads_map, own):
    tokens, width = gated.shape
    n = write.shape[1]
    per = STEP // BLK
    steps = tokens // STEP // 2
    at = (lambda i, s: s[0] * steps + i) if own else (lambda i, s: (1 - s[0]) * steps + i)
    return pl.pallas_call(
        inner_kernel,
        grid_spec=pltpu.PrefetchScalarGridSpec(
            num_scalar_prefetch=1,
            grid=(steps,),
            in_specs=[
                pl.BlockSpec((STEP, n), lambda i, s: (at(i, s), 0)),
                pl.BlockSpec((STEP, n), lambda i, s: (at(i, s), 0)),
                pl.BlockSpec((per, *u.shape[1:]), lambda i, s: (at(i, s), 0, 0)),
                pl.BlockSpec((STEP, width), lambda i, s: (at(i, s), 0)),
                pl.BlockSpec((STEP, width), lambda i, s: (at(i, s), 0)),
                pl.BlockSpec((per, n, width), lambda i, s: (at(i, s), 0, 0)),
                pl.BlockSpec((n, width), lambda i, s: (0, 0)),
                pl.BlockSpec((per, 8, width), lambda i, s: (at(i, s), 0, 0)),
                pl.BlockSpec((1, width), lambda i, s: (0, 0)),
                pl.BlockSpec(heads_map.shape, lambda i, s: (0, 0)),
            ],
            out_specs=pl.BlockSpec((STEP, width), lambda i, s: (i, 0)),
        ),
        out_shape=jax.ShapeDtypeStruct((tokens // 2, width), jnp.bfloat16),
        compiler_params=pltpu.CompilerParams(
            dimension_semantics=("arbitrary",), vmem_limit_bytes=40 * 2**20
        ),
        cost_estimate=pl.CostEstimate(flops=10**9, bytes_accessed=6 * 10**6, transcendentals=0),
        name="inner_own" if own else "inner_other",
    )(info, write, read, u, gated, gated_v, local, inflow, row, skip, heads_map)


def product_kernel(info_ref, own_ref, other_ref, w_ref, base_ref, out_ref, lhs_ref):
    core = info_ref[0]
    width = own_ref.shape[1]

    @pl.when(pl.program_id(0) == 0)
    def _():
        lhs_ref[:, pl.ds(pl.multiple_of(core * width, 128), width)] = own_ref[...]
        lhs_ref[:, pl.ds(pl.multiple_of((1 - core) * width, 128), width)] = other_ref[...]

    value = lax.dot_general(
        lhs_ref[...], w_ref[...], (((1,), (1,)), ((), ())), preferred_element_type=jnp.float32
    )
    out_ref[...] = (base_ref[...].astype(jnp.float32) + value).astype(jnp.bfloat16)


def product(info, own, other, w, base, name):
    rows, width = own.shape
    features = w.shape[0]
    tall = features // 4
    return pl.pallas_call(
        product_kernel,
        grid_spec=pltpu.PrefetchScalarGridSpec(
            num_scalar_prefetch=1,
            grid=(4,),
            in_specs=[
                pl.BlockSpec((rows, width), lambda i, s: (0, 0)),
                pl.BlockSpec((rows, width), lambda i, s: (0, 0)),
                pl.BlockSpec((tall, 2 * width), lambda i, s: (i, 0)),
                pl.BlockSpec((rows, tall), lambda i, s: (0, i)),
            ],
            out_specs=pl.BlockSpec((rows, tall), lambda i, s: (0, i)),
            scratch_shapes=[pltpu.VMEM((rows, 2 * width), jnp.bfloat16)],
        ),
        out_shape=jax.ShapeDtypeStruct((rows, features), jnp.bfloat16),
        compiler_params=pltpu.CompilerParams(
            dimension_semantics=("arbitrary",), vmem_limit_bytes=40 * 2**20
        ),
        cost_estimate=pl.CostEstimate(
            flops=2 * rows * features * 2 * width, bytes_accessed=4 * features * width, transcendentals=0
        ),
        name=name,
    )(info, own, other, w, base)


def pick(left, right):
    return jnp.dot(left, right, preferred_element_type=jnp.float32).astype(jnp.bfloat16)


def body(
    grad_top,
    in_weight,
    out_weight,
    gate_branch,
    write_vec,
    read_vec,
    log_decay,
    step_size,
    skip_gain,
    visual_pos,
    visual_count,
    visual_owner,
    visual_patch,
):
    x_at, z_at, core = lax.axis_index(X), lax.axis_index(Z), lax.axis_index(C)
    seq_count = lax.axis_size(SEQ)
    seq_index = lax.axis_index(SEQ)
    sign = 1 - 2 * core
    grad_rows = grad_top[0]
    tok_rows, model_width = grad_rows.shape
    n = write_vec.shape[2]
    heads = log_decay.shape[1] // 2
    info = jnp.stack([core, x_at, z_at]).astype(jnp.int32)

    rows_y = lax.all_gather(jnp.concatenate([out_weight, in_weight], axis=1), Y, axis=0, tiled=True)
    w_out_rows, w_in_rows = rows_y[:, : out_weight.shape[1]], rows_y[:, out_weight.shape[1] :]
    w_in_full = lax.all_gather(w_in_rows, SEQ, axis=0, tiled=True)

    w_mine = half_of(w_out_rows, core, 1)
    w_other = swap_cores(half_of(w_out_rows, 1 - core, 1))
    w_chip = chip_rows(w_mine, w_other, core)
    part = w_chip.shape[1] // 2
    pieces = []
    places = []
    for color, (first, second) in enumerate(((X, Z), (Z, X))):
        own = w_chip[:, color * part : (color + 1) * part]
        plane = jnp.stack([own] + [send(own, first, s) for s in (1, 2, 3)])
        for k2 in range(4):
            pieces.append(plane)
            if k2 < 3:
                plane = send(plane, second, 1)
            for k1 in range(4):
                kx, kz = (k1, k2) if color == 0 else (k2, k1)
                places.append(lax.rem(x_at - sign * kx + 4, 4) * 4 + lax.rem(z_at - sign * kz + 4, 4))
    place = jnp.stack(places).astype(jnp.int32)

    x_other = swap_cores(grad_rows)
    gate_other = swap_cores(half_of(gate_branch[0], 1 - core, 1))
    vectors = jnp.stack([write_vec[0], read_vec[0]])
    write, read = chip_rows(vectors, swap_cores(vectors), core, axis=1)
    scalars_other = swap_cores(
        jnp.concatenate([half_of(log_decay[0], 1 - core, 0), half_of(step_size[0], 1 - core, 0)])
    )
    skip = jnp.repeat(half_of(skip_gain, core, 0), 64)[None]
    heads_map = jnp.asarray(np.tile(np.repeat(np.eye(heads), 64, axis=1), (2, 1)), jnp.bfloat16)
    u, v, row, extra = decays(info, log_decay[0], step_size[0], scalars_other, heads_map)

    owner_row = visual_owner[0]
    patch_row = visual_patch[0]
    count_row = visual_count[0]
    slot_count = owner_row.shape[1]
    slot_ids = jnp.arange(slot_count)
    live_slot = slot_ids[None, :] < count_row[:, None]
    earlier_slot = slot_ids[None, :] < slot_ids[:, None]
    same_owner = (
        (owner_row[:, :, None] == owner_row[:, None, :])
        & live_slot[:, None, :]
        & earlier_slot[None]
    )
    rank_row = jnp.sum(same_owner.astype(jnp.int32), axis=2)
    own_owner = lax.dynamic_index_in_dim(owner_row, seq_index, 0, keepdims=False)
    own_rank = lax.dynamic_index_in_dim(rank_row, seq_index, 0, keepdims=False)
    own_live = lax.dynamic_index_in_dim(live_slot, seq_index, 0, keepdims=False)
    destination = own_owner * CAP + own_rank
    send_columns = jnp.arange(seq_count * CAP)
    send_map = ((send_columns[:, None] == destination[None, :]) & own_live[None, :]).astype(jnp.bfloat16)
    pos_map = (visual_pos[0, 0][:, None] == jnp.arange(tok_rows)[None, :]).astype(jnp.bfloat16)
    take = jnp.dot(send_map, pos_map, preferred_element_type=jnp.float32).astype(jnp.bfloat16)

    def arrived(sent):
        sent = sent.reshape(seq_count, CAP, sent.shape[1])
        return lax.all_to_all(sent, SEQ, 0, 0, tiled=True).reshape(seq_count * CAP, sent.shape[2])

    def exchange(rows):
        return arrived(pick(take, rows))

    mine_mask = live_slot & (owner_row == seq_index)
    column = jnp.arange(seq_count)[:, None] * CAP + rank_row
    patch_count = seq_count * CAP
    patch_hit = (
        (patch_row.reshape(-1)[:, None] == jnp.arange(patch_count)[None, :])
        & mine_mask.reshape(-1)[:, None]
    ).astype(jnp.bfloat16)
    column_hit = (column.reshape(-1)[:, None] == send_columns[None, :]).astype(jnp.bfloat16)
    select = lax.dot_general(
        patch_hit, column_hit, (((0,), (0,)), ((), ())), preferred_element_type=jnp.float32
    ).astype(jnp.bfloat16)
    placed = lambda rows: jnp.dot(select, rows, preferred_element_type=jnp.float32)

    grad_patches = placed(exchange(grad_rows)).astype(jnp.bfloat16)
    place, grad_patches, take, select = lax.optimization_barrier((place, grad_patches, take, select))

    gated, gated_v, local, share = gated_and_states(
        info, place, pieces, grad_rows, x_other, gate_branch[0], gate_other, read, v, row, extra, heads_map
    )

    share = lax.all_to_all(share, (X, Z), 0, 0, tiled=True)
    inflow = lax.all_to_all(suffix(share, heads_map), (X, Z), 0, 0, tiled=True).reshape(n, -1)
    inner = functools.partial(
        inner_gradient, info, write, read, u, gated, gated_v, local, inflow, row, skip, heads_map
    )
    inner_other = swap_cores(inner(False))
    inner_own = inner(True)

    first = core == 0
    mine, theirs = pick(take, inner_own), pick(take, inner_other)
    rows = jnp.concatenate([jnp.where(first, mine, theirs), jnp.where(first, theirs, mine)], axis=1)
    patch_rows = placed(arrived(rows)).astype(jnp.bfloat16)
    half = patch_rows.shape[1] // 2
    result = product(info, inner_own, inner_other, w_in_full, grad_rows, "product_tokens")
    low, high = patch_rows[:, :half], patch_rows[:, half:]
    patches = product(
        info, jnp.where(first, low, high), jnp.where(first, high, low), w_in_full, grad_patches, "product_patches"
    )
    return (result[None], patches[None])


def solution(mesh):
    finer = Mesh(mesh.devices.reshape(SIZES), ALL)
    return jax.shard_map(
        body,
        mesh=finer,
        in_specs=(
            P(Y, SEQ, None),
            P(ALL, None),
            P(ALL, None),
            P(Y, SEQ, None),
            P(Y, SEQ, None),
            P(Y, SEQ, None),
            P(Y, None, SEQ),
            P(Y, None, SEQ),
            P(),
            P(Y, SEQ, None),
            P(Y, None),
            P(Y, None, None),
            P(Y, None, None),
        ),
        out_specs=(P(Y, SEQ, None), P(Y, SEQ, None)),
        check_vma=False,
    )
```

time: 294 us -> 233 us (0.79)
  other arithmetic: 30.3 us -> 5.62 us
  matrix products: 24.5 us -> 6.34 us
  waiting for transfers between devices: 41.9 us -> 26.7 us
  Pallas kernels: 58.9 us -> 49.3 us
  starting transfers between devices: 50.1 us -> 59 us
  blocking collectives: 48 us -> 41 us
  local copies, waits for them, and re-layouts: 23.5 us -> 29.3 us
    unnamed x1 -> x0, blocking collectives: 33.8 us -> none
    all_to_all x0 -> x2, blocking collectives: none -> 26.7 us  [the longest x1 13.8 us: arrived(): lax.all_to_all(sent, SEQ, 0, 0, tiled=True)]
    dot_general x4 -> x3, matrix products: 22.7 us -> 2 us  [pick(): jnp.dot(left, right, preferred_element_type=jnp.float32)]
    unnamed x50, local copies, waits for them, and re-layouts: 4.17 us -> 16.8 us
    pallas_call x2 -> x6, Pallas kernels: 42.7 us -> 30.9 us  [the longest x2 18.5 us: product(): pl.pallas_call(product_kernel, grid_spec=pltpu.PrefetchScalarGridSpec(num...]
    all_to_all x4 -> x2, waiting for transfers between devices: 17.7 us -> 7.37 us  [the longest x1 7.37 us: body(): lax.all_to_all(suffix(share, heads_map), (X, Z), 0, 0, tiled=True)]
    ppermute x12, starting transfers between devices: 15 us -> 25 us  [send(): return lax.ppermute(a, ALL, ring_perm(axis, shift))]
    unnamed x15 -> x1, other arithmetic: 9.66 us -> 0.98 us
  transfers between devices with their start and end apart: 23 -> 21, of which waited for: 7 -> 4; matrix products, arithmetic and copies ran while one was open for 19% -> 10% of each run, Pallas kernels for 20% -> 13%
where the time goes in v2:
time: 233 us; the launch traced here: 232 us
  starting transfers between devices  59 us (25%)
  Pallas kernels  49.3 us (21%)
  blocking collectives  41 us (18%)
  local copies, waits for them, and re-layouts  29.3 us (13%)
  waiting for transfers between devices  26.7 us (11%)
  between operations  14.4 us (6%)
  matrix products  6.34 us (3%)
  other arithmetic  5.62 us (2%)
    ppermute x12, starting transfers between devices, send(): return lax.ppermute(a, ALL, ring_perm(axis, shift))  25 us
    ppermute x6, starting transfers between devices, swap_cores(): return lax.ppermute(a, C, [(0, 1), (1, 0)])  22.3 us
    ppermute x12, waiting for transfers between devices, send(): return lax.ppermute(a, ALL, ring_perm(axis, shift))  18.9 us
    pallas_call x2, Pallas kernels, product(): pl.pallas_call(product_kernel, grid_spec=pltpu.PrefetchScalarGridSpec(num...  18.5 us
    pallas_call x1, Pallas kernels, gated_and_states(): pl.pallas_call(gated_kernel, grid_spec=pltpu.PrefetchScalarGridSpec(num_s...  18.4 us
    unnamed x50, local copies, waits for them, and re-layouts  16.8 us
    all_gather x1, blocking collectives, body(): lax.all_gather(jnp.concatenate([out_weight, in_weight], axis=1), Y, axis=...  14.2 us
    all_to_all x1, blocking collectives, arrived(): lax.all_to_all(sent, SEQ, 0, 0, tiled=True)  13.8 us
  transfers between devices with their start and end apart: 21, of which 4 were waited for; matrix products, arithmetic and copies ran while one was open for 10% of the time, Pallas kernels for 13%

profile of v2, /device:TPU:1, one launch (start us, length us, event | category | flops | bytes accessed | tf_op | source)
XLA Modules:
  0.0 231.7 jit_solution(3066464840326925531)
XLA Ops:
  8.2 14.2 %all-gather = bf16[4,20,5120]{2,1,0:T(8,128)(2,1)S(1)} all-gather(bf16[1,20,5120]{2,1,0:T(8,128)(2,1)S(1)} %maximum_bitcast_fusion), channel_id=1, replica_groups=mesh['seq_0'=4,'seq_1'=4,'seq_2'=2,'section'=4] {'section'}, dimensions={0}, use_global_device_ids=true | all-gather | bytes 1024000 | tf_op jit(solution)/shard_map/all_gather | solution.py:384
  24.7 2.1 collective-permute-start.2
  31.6 2.5 %collective-permute-start.4 = (bf16[160,640]{1,0:T(8,128)(2,1)S(1)}, bf16[160,640]{1,0:T(8,128)(2,1)S(1)}, u32[]{:S(2)}, u32[]{:S(2)}) collective-permute-start(bf16[160,640]{1,0:T(8,128)(2,1)S(1)} %get-tuple-element.35), channel_id=1, source_target_pairs={{0,64},{1,65},{2,66},{3,67},{4,68},{5,69},{6,70},{7,71},{8,72},{9,... | collective-permute-start | bytes 614408 | tf_op jit(solution)/shard_map/ppermute | solution.py:33
  36.9 3.3 %collective-permute-start.10 = (bf16[160,640]{1,0:T(8,128)(2,1)S(1)}, bf16[160,640]{1,0:T(8,128)(2,1)S(1)}, u32[]{:S(2)}, u32[]{:S(2)}) collective-permute-start(bf16[160,640]{1,0:T(8,128)(2,1)S(1)} %get-tuple-element.34), channel_id=1, source_target_pairs={{0,16},{1,17},{2,18},{3,19},{4,20},{5,21},{6,22},{7,23},{8,24},{9,... | collective-permute-start | bytes 614408 | tf_op jit(solution)/shard_map/ppermute | solution.py:33
  40.9 4.5 %collective-permute-start.1 = (f32[40,512]{1,0:T(8,128)}, f32[40,512]{1,0:T(8,128)}, u32[]{:S(2)}, u32[]{:S(2)}) collective-permute-start(f32[40,512]{1,0:T(8,128)} %pad_maximum_fusion.5), channel_id=1, source_target_pairs={{0,4},{4,0},{1,5},{5,1},{2,6},{6,2},{3,7},{7,3},{8,12},{12,8},{9,1... | collective-permute-start | bytes 245768 | tf_op jit(solution)/shard_map/ppermute | solution.py:37
  46.7 4.4 %collective-permute-start.6 = (bf16[4,160,640]{2,1,0:T(8,128)(2,1)S(1)}, bf16[4,160,640]{2,1,0:T(8,128)(2,1)}, u32[]{:S(2)}, u32[]{:S(2)}) collective-permute-start(bf16[4,160,640]{2,1,0:T(8,128)(2,1)S(1)} %pad_maximum_fusion.refs_0_), channel_id=1, source_target_pairs={{0,8},{1,9},{2,10},{3,11},{4,28},{5,29},{6,30},{7,31},{8,16},{9,17... | collective-permute-start | bytes 2457608 | tf_op jit(solution)/shard_map/ppermute | solution.py:33
  51.1 3.0 %collective-permute-done.10 = bf16[160,640]{1,0:T(8,128)(2,1)S(1)} collective-permute-done((bf16[160,640]{1,0:T(8,128)(2,1)S(1)}, bf16[160,640]{1,0:T(8,128)(2,1)S(1)}, u32[]{:S(2)}, u32[]{:S(2)}) %collective-permute-start.10) | collective-permute-done | bytes 204832 | tf_op jit(solution)/shard_map/ppermute | solution.py:33
  56.7 1.8 reshape.111
  58.5 8.0 %all-to-all-start = ((bf16[32,2,2560]{2,1,0:T(2,128)(2,1)}), bf16[32,2,2560]{2,1,0:T(2,128)(2,1)}, u32[]{:S(2)}, u32[]{:S(2)}) async-start(bf16[32,2,2560]{2,1,0:T(2,128)(2,1)} %reshape.111), calls=%async_computation | async-start | bytes 655360 | tf_op jit(solution)/shard_map/all_to_all | solution.py:441
  66.5 2.5 %dynamic-slice_bitcast_fusion = bf16[512,1280]{1,0:T(8,128)(2,1)} fusion(bf16[1,512,2560]{2,1,0:T(8,128)(2,1)} %param.17, s32[]{:T(128)S(6)} %select_n.72), kind=kLoop, calls=%fused_computation.5 | loop fusion | bytes 2621444 | tf_op jit(solution)/shard_map/dynamic_slice | solution.py:47
  69.3 2.7 %collective-permute-start.7 = (bf16[4,160,640]{2,1,0:T(8,128)(2,1)}, bf16[4,160,640]{2,1,0:T(8,128)(2,1)}, u32[]{:S(2)}, u32[]{:S(2)}) collective-permute-start(bf16[4,160,640]{2,1,0:T(8,128)(2,1)} %collective-permute-done.6.refs_1_), channel_id=1, source_target_pairs={{0,8},{1,9},{2,10},{3,11},{4,28},{5,29},{6,30},{7,31},{8,16},{9,17... | collective-permute-start | bytes 2457608 | tf_op jit(solution)/shard_map/ppermute | solution.py:33
  72.0 2.5 %collective-permute-start.13 = (bf16[4,160,640]{2,1,0:T(8,128)(2,1)}, bf16[4,160,640]{2,1,0:T(8,128)(2,1)}, u32[]{:S(2)}, u32[]{:S(2)}) collective-permute-start(bf16[4,160,640]{2,1,0:T(8,128)(2,1)} %collective-permute-done.12.refs_5_), channel_id=1, source_target_pairs={{0,32},{1,33},{2,34},{3,35},{4,100},{5,101},{6,102},{7,103},{8,40}... | collective-permute-start | bytes 2457608 | tf_op jit(solution)/shard_map/ppermute | solution.py:33
  77.4 5.5 %collective-permute-start = (bf16[2,512,128]{2,1,0:T(8,128)(2,1)S(1)}, bf16[2,512,128]{2,1,0:T(8,128)(2,1)S(1)}, u32[]{:S(2)}, u32[]{:S(2)}) collective-permute-start(bf16[2,512,128]{2,1,0:T(8,128)(2,1)S(1)} %constant_dynamic-update-slice_fusion), channel_id=1, source_target_pairs={{0,4},{4,0},{1,5},{5,1},{2,6},{6,2},{3,7},{7,3},{8,12},{12,8},{9,1... | collective-permute-start | bytes 786440 | tf_op jit(solution)/shard_map/ppermute | solution.py:37
  82.9 1.9 convolution_convert_fusion.6
  85.0 15.9 %collective-permute-done.7.refs_2_ = bf16[4,160,640]{2,1,0:T(8,128)(2,1)} collective-permute-done((bf16[4,160,640]{2,1,0:T(8,128)(2,1)}, bf16[4,160,640]{2,1,0:T(8,128)(2,1)}, u32[]{:S(2)}, u32[]{:S(2)}) %collective-permute-start.7) | collective-permute-done | bytes 819232 | tf_op jit(solution)/shard_map/ppermute | solution.py:33
  100.9 3.2 %collective-permute-start.8 = (bf16[4,160,640]{2,1,0:T(8,128)(2,1)}, bf16[4,160,640]{2,1,0:T(8,128)(2,1)}, u32[]{:S(2)}, u32[]{:S(2)}) collective-permute-start(bf16[4,160,640]{2,1,0:T(8,128)(2,1)} %collective-permute-done.7.refs_2_), channel_id=1, source_target_pairs={{0,8},{1,9},{2,10},{3,11},{4,28},{5,29},{6,30},{7,31},{8,16},{9,17... | collective-permute-start | bytes 2457608 | tf_op jit(solution)/shard_map/ppermute | solution.py:33
  106.3 5.9 %decays.1 = (bf16[8,40,128]{2,1,0:T(8,128)(2,1)}, bf16[8,40,128]{2,1,0:T(8,128)(2,1)}, f32[8,8,1280]{2,1,0:T(8,128)}, bf16[8,128]{1,0:T(8,128)(2,1)}) custom-call(s32[3]{0:T(128)} %pad_add_fusion.info_ref, f32[40,512]{1,0:T(8,128)} %bitcast.86, f32[40,512]{1,0:T(8,128)} %bitcast.87, f32[40,512]{1,0:T(8,128)} %collective-permute-done.1.other_ref, ...), custom_call_target="tpu_custom_call" | custom-call | flops 1000000000 | bytes 1000000 | tf_op jit(solution)/shard_map/decays/pallas_call | solution.py:106
  112.4 1.8 reshape.112
  114.2 2.0 convolution_convert_fusion.2.base_ref
  119.2 18.4 %gated.1 = (bf16[1024,1280]{1,0:T(8,128)(2,1)}, bf16[1024,1280]{1,0:T(8,128)(2,1)}, bf16[8,128,1280]{2,1,0:T(8,128)(2,1)}, bf16[16,8,1408]{2,1,0:T(8,128)(2,1)S(1)}) custom-call(s32[3]{0:T(128)S(1)} %copy-done.15, s32[32]{0:T(128)S(1)} %stack.133.place_ref, bf16[4,160,640]{2,1,0:T(8,128)(2,1)S(1)} %copy-done.13, ...), custom_call_target="tpu_custom_call" | custom-call | flops 8000000000 | bytes 24000000 | tf_op jit(solution)/shard_map/gated/pallas_call | solution.py:191
  137.6 13.0 %all_to_all.20.share_ref = bf16[16,8,1408]{2,1,0:T(8,128)(2,1)} all-to-all(bf16[16,8,1408]{2,1,0:T(8,128)(2,1)S(1)} %get-tuple-element.22), channel_id=1, replica_groups=mesh['seq_0'=4,'seq_1'=4,'seq_2'=2,'section'=4] {'seq_0','seq_1'}, dimensions={0} | all-to-all | bytes 720896 | tf_op jit(solution)/shard_map/all_to_all | solution.py:466
  150.5 2.0 suffix.1
  152.5 3.5 %all-to-all-start.2 = ((bf16[16,8,1280]{2,1,0:T(8,128)(2,1)}), bf16[16,8,1280]{2,1,0:T(8,128)(2,1)S(1)}, u32[]{:S(2)}, u32[]{:S(2)}) async-start(bf16[16,8,1280]{2,1,0:T(8,128)(2,1)} %suffix.1), calls=%async_computation.2 | async-start | bytes 655360 | tf_op jit(solution)/shard_map/all_to_all | solution.py:467
  156.3 7.4 %all-to-all-done.2 = bf16[16,8,1280]{2,1,0:T(8,128)(2,1)S(1)} async-done(((bf16[16,8,1280]{2,1,0:T(8,128)(2,1)}), bf16[16,8,1280]{2,1,0:T(8,128)(2,1)S(1)}, u32[]{:S(2)}, u32[]{:S(2)}) %all-to-all-start.2) | async-done | bytes 327712 | tf_op jit(solution)/shard_map/all_to_all | solution.py:467
  163.7 1.7 copy-done.1
  168.9 2.3 inner_other.1
  171.2 8.9 %collective-permute-start.17 = (bf16[512,1280]{1,0:T(8,128)(2,1)S(1)}, bf16[512,1280]{1,0:T(8,128)(2,1)S(1)}, u32[]{:S(2)}, u32[]{:S(2)}) collective-permute-start(bf16[512,1280]{1,0:T(8,128)(2,1)S(1)} %inner_other.1), channel_id=1, source_target_pairs={{0,4},{4,0},{1,5},{5,1},{2,6},{6,2},{3,7},{7,3},{8,12},{12,8},{9,1... | collective-permute-start | bytes 3932168 | tf_op jit(solution)/shard_map/ppermute | solution.py:37
  180.1 2.3 inner_own.1.own_ref
  184.7 13.8 %all_to_all.21 = bf16[32,2,2560]{2,1,0:T(2,128)(2,1)} all-to-all(bf16[32,2,2560]{2,1,0:T(2,128)(2,1)S(1)} %reshape.114), channel_id=1, replica_groups=mesh['seq_0'=4,'seq_1'=4,'seq_2'=2,'section'=4] {'seq_0','seq_1','seq_2'}, dimensions={0} | all-to-all | bytes 655360 | tf_op jit(solution)/shard_map/all_to_all | solution.py:441
  201.6 12.6 %product_tokens.1 = bf16[512,2560]{1,0:T(8,128)(2,1)} custom-call(s32[3]{0:T(128)S(1)} %copy-done.15, bf16[512,1280]{1,0:T(8,128)(2,1)S(1)} %inner_own.1.own_ref, bf16[512,1280]{1,0:T(8,128)(2,1)S(1)} %copy-done.9, bf16[2560,2560]{1,0:T(8,128)(2,1)} %all-gather.3.cloned.1.call-done.w_ref, bf16[512,2560]{1,0:T(8,128)(2,1)S(1)} %bitcast.74), custom_call_target="tpu_custom_call" | custom-call | flops 6710886400 | bytes 13107200 | tf_op jit(solution)/shard_map/product_tokens/pallas_call | solution.py:330
  214.2 4.7 %copy-done = bf16[2560,2560]{1,0:T(8,128)(2,1)S(1)} copy-done((bf16[2560,2560]{1,0:T(8,128)(2,1)S(1)}, bf16[2560,2560]{1,0:T(8,128)(2,1)}, u32[]{:S(2)}) %copy-start) | copy-done | bytes 13107224
  219.0 5.9 %product_patches.1 = bf16[64,2560]{1,0:T(8,128)(2,1)} custom-call(s32[3]{0:T(128)S(1)} %copy-done.15, bf16[64,1280]{1,0:T(8,128)(2,1)S(1)} %get-tuple-element.37.own_ref, bf16[64,1280]{1,0:T(8,128)(2,1)S(1)} %get-tuple-element.36.other_ref, bf16[2560,2560]{1,0:T(8,128)(2,1)S(1)} %copy-done, bf16[64,2560]{1,0:T(8,128)(2,1)S(1)} %copy-done.7), custom_call_target="tpu_custom_call" | custom-call | flops 838860800 | bytes 13107200 | tf_op jit(solution)/shard_map/product_patches/pallas_call | solution.py:330
  (115 shorter events, 33.2 us)
Async XLA Ops:
  7.2 192.7 %all-gather.3.cloned.1.call-start = ((), (), s32[]{:S(2)}) async-start(), calls=%async_computation.4 | async-start | bytes 13516800 | tf_op jit(solution)/shard_map/all_gather | solution.py:386
  8.2 18.5 %copy-start.20 = (f32[1,40,512]{2,1,0:T(8,128)S(1)}, f32[1,40,512]{2,1,0:T(8,128)}, u32[]{:S(2)}) copy-start(f32[1,40,512]{2,1,0:T(8,128)} %param.20) | copy-start | bytes 245764
  8.2 19.4 %copy-start.21 = (s32[1,32]{1,0:T(1,128)S(1)}, s32[1,32]{1,0:T(1,128)}, u32[]{:S(2)}) copy-start(s32[1,32]{1,0:T(1,128)} %param.24) | copy-start | bytes 388
  8.2 19.5 %copy-start.18 = (s32[1,32,64]{2,1,0:T(8,128)S(1)}, s32[1,32,64]{2,1,0:T(8,128)}, u32[]{:S(2)}) copy-start(s32[1,32,64]{2,1,0:T(8,128)} %param.25) | copy-start | bytes 24580
  22.7 22.8 %copy-start.4 = (bf16[1,512,2560]{2,1,0:T(8,128)(2,1)S(1)}, bf16[1,512,2560]{2,1,0:T(8,128)(2,1)}, u32[]{:S(2)}) copy-start(bf16[1,512,2560]{2,1,0:T(8,128)(2,1)} %param.14) | copy-start | bytes 7864324
  24.7 4.0 %collective-permute-start.2 = (bf16[80,1280]{1,0:T(8,128)(2,1)S(1)}, bf16[80,1280]{1,0:T(8,128)(2,1)S(1)}, u32[]{:S(2)}, u32[]{:S(2)}) collective-permute-start(bf16[80,1280]{1,0:T(8,128)(2,1)S(1)} %constant_dynamic-slice_fusion), channel_id=1, source_target_pairs={{0,4},{4,0},{1,5},{5,1},{2,6},{6,2},{3,7},{7,3},{8,12},{12,8},{9,1... | collective-permute-start | bytes 614408 | tf_op jit(solution)/shard_map/ppermute | solution.py:37
  27.6 27.6 %copy-start.22 = (s32[1,1,64]{2,1,0:T(1,128)S(1)}, s32[1,1,64]{2,1,0:T(1,128)}, u32[]{:S(2)}) copy-start(s32[1,1,64]{2,1,0:T(1,128)} %param.23) | copy-start | bytes 772
  29.7 10.5 %collective-permute-start.5 = (bf16[160,640]{1,0:T(8,128)(2,1)S(1)}, bf16[160,640]{1,0:T(8,128)(2,1)S(1)}, u32[]{:S(2)}, u32[]{:S(2)}) collective-permute-start(bf16[160,640]{1,0:T(8,128)(2,1)S(1)} %get-tuple-element.35), channel_id=1, source_target_pairs={{0,96},{1,97},{2,98},{3,99},{4,36},{5,37},{6,38},{7,39},{8,104},{9... | collective-permute-start | bytes 614408 | tf_op jit(solution)/shard_map/ppermute | solution.py:33
  31.6 9.3 %collective-permute-start.4 = (bf16[160,640]{1,0:T(8,128)(2,1)S(1)}, bf16[160,640]{1,0:T(8,128)(2,1)S(1)}, u32[]{:S(2)}, u32[]{:S(2)}) collective-permute-start(bf16[160,640]{1,0:T(8,128)(2,1)S(1)} %get-tuple-element.35), channel_id=1, source_target_pairs={{0,64},{1,65},{2,66},{3,67},{4,68},{5,69},{6,70},{7,71},{8,72},{9,... | collective-permute-start | bytes 614408 | tf_op jit(solution)/shard_map/ppermute | solution.py:33
  34.1 11.4 %collective-permute-start.3 = (bf16[160,640]{1,0:T(8,128)(2,1)S(1)}, bf16[160,640]{1,0:T(8,128)(2,1)S(1)}, u32[]{:S(2)}, u32[]{:S(2)}) collective-permute-start(bf16[160,640]{1,0:T(8,128)(2,1)S(1)} %get-tuple-element.35), channel_id=1, source_target_pairs={{0,32},{1,33},{2,34},{3,35},{4,100},{5,101},{6,102},{7,103},{8,40}... | collective-permute-start | bytes 614408 | tf_op jit(solution)/shard_map/ppermute | solution.py:33
  35.2 11.4 %collective-permute-start.11 = (bf16[160,640]{1,0:T(8,128)(2,1)S(1)}, bf16[160,640]{1,0:T(8,128)(2,1)S(1)}, u32[]{:S(2)}, u32[]{:S(2)}) collective-permute-start(bf16[160,640]{1,0:T(8,128)(2,1)S(1)} %get-tuple-element.34), channel_id=1, source_target_pairs={{0,24},{1,25},{2,26},{3,27},{4,12},{5,13},{6,14},{7,15},{8,0},{9,1... | collective-permute-start | bytes 614408 | tf_op jit(solution)/shard_map/ppermute | solution.py:33
  36.9 17.2 %collective-permute-start.10 = (bf16[160,640]{1,0:T(8,128)(2,1)S(1)}, bf16[160,640]{1,0:T(8,128)(2,1)S(1)}, u32[]{:S(2)}, u32[]{:S(2)}) collective-permute-start(bf16[160,640]{1,0:T(8,128)(2,1)S(1)} %get-tuple-element.34), channel_id=1, source_target_pairs={{0,16},{1,17},{2,18},{3,19},{4,20},{5,21},{6,22},{7,23},{8,24},{9,... | collective-permute-start | bytes 614408 | tf_op jit(solution)/shard_map/ppermute | solution.py:33
  40.2 13.9 %collective-permute-start.9 = (bf16[160,640]{1,0:T(8,128)(2,1)S(1)}, bf16[160,640]{1,0:T(8,128)(2,1)S(1)}, u32[]{:S(2)}, u32[]{:S(2)}) collective-permute-start(bf16[160,640]{1,0:T(8,128)(2,1)S(1)} %get-tuple-element.34), channel_id=1, source_target_pairs={{0,8},{1,9},{2,10},{3,11},{4,28},{5,29},{6,30},{7,31},{8,16},{9,17... | collective-permute-start | bytes 614408 | tf_op jit(solution)/shard_map/ppermute | solution.py:33
  40.9 36.5 %collective-permute-start.1 = (f32[40,512]{1,0:T(8,128)}, f32[40,512]{1,0:T(8,128)}, u32[]{:S(2)}, u32[]{:S(2)}) collective-permute-start(f32[40,512]{1,0:T(8,128)} %pad_maximum_fusion.5), channel_id=1, source_target_pairs={{0,4},{4,0},{1,5},{5,1},{2,6},{6,2},{3,7},{7,3},{8,12},{12,8},{9,1... | collective-permute-start | bytes 245768 | tf_op jit(solution)/shard_map/ppermute | solution.py:37
  45.4 70.7 %collective-permute-start.15 = (bf16[512,2560]{1,0:T(8,128)(2,1)S(1)}, bf16[512,2560]{1,0:T(8,128)(2,1)}, u32[]{:S(2)}, u32[]{:S(2)}) collective-permute-start(bf16[512,2560]{1,0:T(8,128)(2,1)S(1)} %bitcast.73), channel_id=1, source_target_pairs={{0,4},{4,0},{1,5},{5,1},{2,6},{6,2},{3,7},{7,3},{8,12},{12,8},{9,1... | collective-permute-start | bytes 7864328 | tf_op jit(solution)/shard_map/ppermute | solution.py:37
  46.7 22.6 %collective-permute-start.6 = (bf16[4,160,640]{2,1,0:T(8,128)(2,1)S(1)}, bf16[4,160,640]{2,1,0:T(8,128)(2,1)}, u32[]{:S(2)}, u32[]{:S(2)}) collective-permute-start(bf16[4,160,640]{2,1,0:T(8,128)(2,1)S(1)} %pad_maximum_fusion.refs_0_), channel_id=1, source_target_pairs={{0,8},{1,9},{2,10},{3,11},{4,28},{5,29},{6,30},{7,31},{8,16},{9,17... | collective-permute-start | bytes 2457608 | tf_op jit(solution)/shard_map/ppermute | solution.py:33
  55.1 16.8 %collective-permute-start.12 = (bf16[4,160,640]{2,1,0:T(8,128)(2,1)}, bf16[4,160,640]{2,1,0:T(8,128)(2,1)}, u32[]{:S(2)}, u32[]{:S(2)}) collective-permute-start(bf16[4,160,640]{2,1,0:T(8,128)(2,1)} %pad_maximum_fusion.1.refs_4_), channel_id=1, source_target_pairs={{0,32},{1,33},{2,34},{3,35},{4,100},{5,101},{6,102},{7,103},{8,40}... | collective-permute-start | bytes 2457608 | tf_op jit(solution)/shard_map/ppermute | solution.py:33
  58.5 53.8 %all-to-all-start = ((bf16[32,2,2560]{2,1,0:T(2,128)(2,1)}), bf16[32,2,2560]{2,1,0:T(2,128)(2,1)}, u32[]{:S(2)}, u32[]{:S(2)}) async-start(bf16[32,2,2560]{2,1,0:T(2,128)(2,1)} %reshape.111), calls=%async_computation | async-start | bytes 655360 | tf_op jit(solution)/shard_map/all_to_all | solution.py:441
  69.0 47.2 %collective-permute-start.16 = (bf16[512,1280]{1,0:T(8,128)(2,1)}, bf16[512,1280]{1,0:T(8,128)(2,1)}, u32[]{:S(2)}, u32[]{:S(2)}) collective-permute-start(bf16[512,1280]{1,0:T(8,128)(2,1)} %dynamic-slice_bitcast_fusion), channel_id=1, source_target_pairs={{0,4},{4,0},{1,5},{5,1},{2,6},{6,2},{3,7},{7,3},{8,12},{12,8},{9,1... | collective-permute-start | bytes 3932168 | tf_op jit(solution)/shard_map/ppermute | solution.py:37
  69.3 31.6 %collective-permute-start.7 = (bf16[4,160,640]{2,1,0:T(8,128)(2,1)}, bf16[4,160,640]{2,1,0:T(8,128)(2,1)}, u32[]{:S(2)}, u32[]{:S(2)}) collective-permute-start(bf16[4,160,640]{2,1,0:T(8,128)(2,1)} %collective-permute-done.6.refs_1_), channel_id=1, source_target_pairs={{0,8},{1,9},{2,10},{3,11},{4,28},{5,29},{6,30},{7,31},{8,16},{9,17... | collective-permute-start | bytes 2457608 | tf_op jit(solution)/shard_map/ppermute | solution.py:33
  72.0 32.1 %collective-permute-start.13 = (bf16[4,160,640]{2,1,0:T(8,128)(2,1)}, bf16[4,160,640]{2,1,0:T(8,128)(2,1)}, u32[]{:S(2)}, u32[]{:S(2)}) collective-permute-start(bf16[4,160,640]{2,1,0:T(8,128)(2,1)} %collective-permute-done.12.refs_5_), channel_id=1, source_target_pairs={{0,32},{1,33},{2,34},{3,35},{4,100},{5,101},{6,102},{7,103},{8,40}... | collective-permute-start | bytes 2457608 | tf_op jit(solution)/shard_map/ppermute | solution.py:33
  77.4 34.8 %collective-permute-start = (bf16[2,512,128]{2,1,0:T(8,128)(2,1)S(1)}, bf16[2,512,128]{2,1,0:T(8,128)(2,1)S(1)}, u32[]{:S(2)}, u32[]{:S(2)}) collective-permute-start(bf16[2,512,128]{2,1,0:T(8,128)(2,1)S(1)} %constant_dynamic-update-slice_fusion), channel_id=1, source_target_pairs={{0,4},{4,0},{1,5},{5,1},{2,6},{6,2},{3,7},{7,3},{8,12},{12,8},{9,1... | collective-permute-start | bytes 786440 | tf_op jit(solution)/shard_map/ppermute | solution.py:37
  100.9 15.3 %collective-permute-start.8 = (bf16[4,160,640]{2,1,0:T(8,128)(2,1)}, bf16[4,160,640]{2,1,0:T(8,128)(2,1)}, u32[]{:S(2)}, u32[]{:S(2)}) collective-permute-start(bf16[4,160,640]{2,1,0:T(8,128)(2,1)} %collective-permute-done.7.refs_2_), channel_id=1, source_target_pairs={{0,8},{1,9},{2,10},{3,11},{4,28},{5,29},{6,30},{7,31},{8,16},{9,17... | collective-permute-start | bytes 2457608 | tf_op jit(solution)/shard_map/ppermute | solution.py:33
  104.1 12.1 %collective-permute-start.14 = (bf16[4,160,640]{2,1,0:T(8,128)(2,1)}, bf16[4,160,640]{2,1,0:T(8,128)(2,1)}, u32[]{:S(2)}, u32[]{:S(2)}) collective-permute-start(bf16[4,160,640]{2,1,0:T(8,128)(2,1)} %collective-permute-done.13.refs_6_), channel_id=1, source_target_pairs={{0,32},{1,33},{2,34},{3,35},{4,100},{5,101},{6,102},{7,103},{8,40}... | collective-permute-start | bytes 2457608 | tf_op jit(solution)/shard_map/ppermute | solution.py:33
  119.1 36.9 %copy-start.23 = (f32[40]{0:T(128)S(1)}, f32[40]{0:T(128)}, u32[]{:S(2)}) copy-start(f32[40]{0:T(128)} %param.22) | copy-start | bytes 484
  119.1 44.5 %copy-start.11 = (bf16[40,1280]{1,0:T(8,128)(2,1)S(1)}, bf16[40,1280]{1,0:T(8,128)(2,1)}, u32[]{:S(2)}) copy-start(bf16[40,1280]{1,0:T(8,128)(2,1)} %constant.69.clone.heads_ref.refs_16_) | copy-start | bytes 307204
  119.2 44.5 %copy-start.14 = (bf16[8,40,128]{2,1,0:T(8,128)(2,1)S(1)}, bf16[8,40,128]{2,1,0:T(8,128)(2,1)}, u32[]{:S(2)}) copy-start(bf16[8,40,128]{2,1,0:T(8,128)(2,1)} %get-tuple-element.14.u_ref) | copy-start | bytes 245764
  152.5 11.2 %all-to-all-start.2 = ((bf16[16,8,1280]{2,1,0:T(8,128)(2,1)}), bf16[16,8,1280]{2,1,0:T(8,128)(2,1)S(1)}, u32[]{:S(2)}, u32[]{:S(2)}) async-start(bf16[16,8,1280]{2,1,0:T(8,128)(2,1)} %suffix.1), calls=%async_computation.2 | async-start | bytes 655360 | tf_op jit(solution)/shard_map/all_to_all | solution.py:467
  171.2 11.6 %collective-permute-start.17 = (bf16[512,1280]{1,0:T(8,128)(2,1)S(1)}, bf16[512,1280]{1,0:T(8,128)(2,1)S(1)}, u32[]{:S(2)}, u32[]{:S(2)}) collective-permute-start(bf16[512,1280]{1,0:T(8,128)(2,1)S(1)} %inner_other.1), channel_id=1, source_target_pairs={{0,4},{4,0},{1,5},{5,1},{2,6},{6,2},{3,7},{7,3},{8,12},{12,8},{9,1... | collective-permute-start | bytes 3932168 | tf_op jit(solution)/shard_map/ppermute | solution.py:37
  184.2 15.4 %copy-start.19 = (bf16[64,64]{1,0:T(8,128)(2,1)S(1)}, bf16[64,64]{1,0:T(8,128)(2,1)}, u32[]{:S(2)}) copy-start(bf16[64,64]{1,0:T(8,128)(2,1)} %convolution_convert_fusion.6) | copy-start | bytes 24580
  184.5 15.3 %copy-start.9 = (bf16[512,1280]{1,0:T(8,128)(2,1)S(1)}, bf16[512,1280]{1,0:T(8,128)(2,1)}, u32[]{:S(2)}) copy-start(bf16[512,1280]{1,0:T(8,128)(2,1)} %copy-done.8) | copy-start | bytes 3932164
  201.6 12.6 %copy-start.7 = (bf16[64,2560]{1,0:T(8,128)(2,1)S(1)}, bf16[64,2560]{1,0:T(8,128)(2,1)}, u32[]{:S(2)}) copy-start(bf16[64,2560]{1,0:T(8,128)(2,1)} %convolution_convert_fusion.2.base_ref) | copy-start | bytes 983044
  (13 other events, 39.4 us)
Sparse Core Ops, SparseCore 0:
  23.8 87.7 all-gather.2
